TPU v7x, 128 devices: a whole 4x4x4 slice. The times are simulated.
128 devices in a mesh: curve: 128 (over y, z, x, core).
Axes of the slice: x: 4, y: 4, z: 4, core: 2. Of those that a mesh axis runs over, the one named last changes fastest.
Arguments:
- nodal_state: float32 [5, 64, 65536], P(None, None, 'curve'), may hold values from -9 to 9, as said below
- inverse_jacobian: float32 [65536], P('curve'), may hold values from 1 to 4
- speeds: float32 [3, 5], replicated, may hold values from -1.5 to 1.5
- refine_flags: int32 [65536], P('curve'), may hold values from 0 to 1, as said below
- send_index: int32 [49152], P('curve'), may hold values from 0 to 3071, as said below
- face_source: int32 [6, 65536], P(None, 'curve'), may hold values from 0 to 3455, as said below
Outputs:
- refined_state: float32 [5, 64, 122880], P(None, None, 'curve')
- refined_jacobian: float32 [122880], P('curve')
Inputs may be any that keep to these rules, and one draw needn't show every extreme that they name: `nodal_state`: each element's 64 node values are a level plus a linear part plus noise of an amplitude that varies from element to element. `refine_flags`: exactly 64 flags per device on average over all devices, at most 128 on one device, a number that is reached; the refined elements of a device go only to itself and its two curve neighbours, at most 224 to each neighbour, a number that is reached. `send_index`: per device, four blocks of 96 entries for destination offsets -2, -1, 1, 2 along the curve (cyclically): entries f * 512 + n of the traces that device reads, in increasing order, then zeros in unused slots; the blocks for offsets -1 and 1 are always full. `face_source`: face pairing is symmetric: across face 2 d of an element lies face 2 d + 1 of its neighbour; neighbours are on the same device or on one within two curve offsets.
All inputs are finite; a program needn't handle non-finite values.
Results may differ from a plain program's by a relative error of at most 0.0003.
Values sent between devices are 32-bit elements; how exact they have to be, the bound alone decides.
A program may use at most 64 MiB of HBM per device.

v0:
```python
import functools
import math

import jax
import jax.numpy as jnp
import numpy as np
from jax import lax
from jax.experimental import pallas as pl
from jax.experimental.pallas import tpu as pltpu
from jax.sharding import PartitionSpec as P

TIME_STEP = 0.02
VARS = 5
E_DEV = 512
E_NEW = 960
SLOTS = 96
ROWS = 64 * VARS
LANES = 128
GROUPS = E_DEV // LANES
ROW_OF = 8
COL_OF = 16
F32 = jnp.float32
BF16 = jnp.bfloat16
MESH = pl.DeviceIdType.MESH


def lagrange_at(points, targets):
    values_at = np.ones((len(targets), 4))
    for basis_id in range(4):
        for partner in range(4):
            if partner != basis_id:
                values_at[:, basis_id] *= (targets - points[partner]) / (
                    points[basis_id] - points[partner]
                )
    return values_at


def tables():
    root = 1.0 / math.sqrt(5.0)
    points = np.array([-1.0, -root, root, 1.0])
    weights = np.array([1.0, 5.0, 5.0, 1.0]) / 6.0
    bary = np.ones(4)
    for a in range(4):
        for b in range(4):
            if a != b:
                bary[a] /= points[a] - points[b]
    deriv = np.zeros((4, 4))
    for a in range(4):
        for b in range(4):
            if a != b:
                deriv[a, b] = bary[b] / bary[a] / (points[a] - points[b])
        deriv[a, a] = -np.sum(deriv[a])
    skew = weights[:, None] * deriv
    legendre = np.stack(
        [points**0, points, 0.5 * (3 * points**2 - 1), 0.5 * (5 * points**3 - 3 * points)], axis=1
    )
    to_modes = np.linalg.inv(legendre)
    sides = [lagrange_at(points, (points - 1.0) / 2.0), lagrange_at(points, (points + 1.0) / 2.0)]
    return skew, np.kron(to_modes, np.kron(to_modes, to_modes)), sides


SKEW, MODES, SIDES = tables()
Q01, Q02, Q03, Q12 = (float(SKEW[0, 1]), float(SKEW[0, 2]), float(SKEW[0, 3]), float(SKEW[1, 2]))
END, MID = 6.0, 1.2


def split2(x):
    high = x.astype(BF16)
    return high, (x - high.astype(F32)).astype(BF16)


def low_half(shape):
    return (lax.broadcasted_iota(jnp.int32, shape, 0) & 7) < 4


def turn(x):
    return pltpu.roll(x, 4, 0)


def fetch_state(x_ref, tile_ref, sems):
    copies = []
    for g in range(GROUPS):
        copy = pltpu.make_async_copy(
            x_ref.at[:, g * LANES : (g + 1) * LANES], tile_ref.at[g], sems.at[g]
        )
        copy.start()
        copies.append(copy)
    return copies


def build_traces(tile_ref, trace_ref, g):
    low = low_half((8, LANES))
    cols = slice(g * LANES, (g + 1) * LANES)
    for v in range(VARS):
        base = 64 * v
        tiles = [tile_ref[g, base + 8 * t : base + 8 * t + 8, :] for t in range(8)]
        first, last = tiles[0::2], tiles[1::2]
        sets = {
            0: [tile_ref[g, pl.ds(base + 32 * h, 8, stride=4), :] for h in range(2)],
            1: [tile_ref[g, pl.ds(base + 32 * h + 3, 8, stride=4), :] for h in range(2)],
            2: [jnp.where(low, first[k], turn(first[k + 1])) for k in (0, 2)],
            3: [jnp.where(low, turn(last[k]), last[k + 1]) for k in (0, 2)],
            4: tiles[0:2],
            5: tiles[6:8],
        }
        for f, rows in sets.items():
            high, rest = split2(jnp.concatenate(rows, axis=0))
            trace_ref[f, 16 * v : 16 * v + 16, cols] = high
            trace_ref[f, 80 + 16 * v : 96 + 16 * v, cols] = rest


def one_hot(index, size, width):
    rows = lax.broadcasted_iota(jnp.int32, (size, width), 0)
    return jnp.where(rows == index, 1.0, 0.0).astype(BF16)


def gather_sends(send_ref, trace_ref, out_ref):
    packed = jnp.broadcast_to(send_ref[...], (8, 4 * SLOTS))
    for block in range(4):
        shift = (4 * SLOTS - SLOTS * block) % (4 * SLOTS)
        moved = packed if shift == 0 else pltpu.roll(packed, shift, 1)
        index = moved[0:1, 0:LANES]
        total = jnp.zeros((160, LANES), F32)
        for f in range(6):
            total = total + jnp.dot(
                trace_ref[f],
                one_hot(index - f * E_DEV, E_DEV, LANES),
                preferred_element_type=F32,
            )
        out_ref[block] = total[0:80] + total[80:160]


def halo_kernel(
    x_ref, send_ref, flag_ref, ghost_ref, before_ref,
    tile_ref, trace_ref, out_buf, row_buf, col_buf, mine, group,
    fetch_sems, send_sems, recv_sems, row_send, row_recv, col_send, col_recv,
):
    fetches = fetch_state(x_ref, tile_ref, fetch_sems)
    me = lax.axis_index("curve")
    devices = ROW_OF * COL_OF
    row_at = me % ROW_OF
    col_at = me // ROW_OF
    offsets = (-2, -1, 1, 2)
    near = [(me + devices + o) % devices for o in offsets]
    row_mates = [col_at * ROW_OF + (row_at + k) % ROW_OF for k in range(1, ROW_OF)]
    col_mates = [((col_at + k) % COL_OF) * ROW_OF + row_at for k in range(1, COL_OF)]
    partners = near + row_mates + col_mates
    barrier = pltpu.get_barrier_semaphore()
    for partner in partners:
        pl.semaphore_signal(barrier, inc=1, device_id=(partner,), device_id_type=MESH)

    count = jnp.sum(flag_ref[...].astype(F32), axis=1, keepdims=True)
    mine[...] = jnp.broadcast_to(count - 64.0, (1, LANES))
    for g in range(GROUPS):
        fetches[g].wait()
        build_traces(tile_ref, trace_ref, g)
    gather_sends(send_ref, trace_ref, out_buf)

    pl.semaphore_wait(barrier, len(partners))
    row_copies = []
    for k, mate in enumerate(row_mates):
        copy = pltpu.make_async_remote_copy(
            src_ref=mine, dst_ref=row_buf.at[k], send_sem=row_send.at[k], recv_sem=row_recv.at[k],
            device_id=(mate,), device_id_type=MESH,
        )
        copy.start()
        row_copies.append(copy)
    copies = []
    for block, mate in enumerate(near):
        copy = pltpu.make_async_remote_copy(
            src_ref=out_buf.at[block], dst_ref=ghost_ref.at[3 - block],
            send_sem=send_sems.at[block], recv_sem=recv_sems.at[3 - block],
            device_id=(mate,), device_id_type=MESH,
        )
        copy.start()
        copies.append(copy)
    for copy in row_copies:
        copy.wait()
    total = mine[...]
    behind = jnp.zeros((1, LANES), F32)
    for k in range(ROW_OF - 1):
        value = row_buf[k]
        total = total + value
        behind = behind + jnp.where(row_at >= k + 1, value, 0.0)
    group[...] = total
    col_copies = []
    for k, mate in enumerate(col_mates):
        copy = pltpu.make_async_remote_copy(
            src_ref=group, dst_ref=col_buf.at[k], send_sem=col_send.at[k], recv_sem=col_recv.at[k],
            device_id=(mate,), device_id_type=MESH,
        )
        copy.start()
        col_copies.append(copy)
    for copy in col_copies:
        copy.wait()
    for k in range(COL_OF - 1):
        behind = behind + jnp.where(col_at >= k + 1, col_buf[k], 0.0)
    before_ref[...] = jnp.broadcast_to(behind, (8, LANES))
    for block in range(4):
        copies[block].wait_send()
        copies[3 - block].wait_recv()


def pair_sum(ui, um, si, sm):
    return (si + sm) + ui * um


def line_update(u, coef):
    ca, cb, c02, c03, cd = coef
    s = [x * x for x in u]
    m = [jnp.abs(x) for x in u]
    e = []
    for n, c in ((0, ca), (1, cb), (2, ca)):
        g = pair_sum(u[n], u[n + 1], s[n], s[n + 1])
        e.append(c * g - cd * (jnp.maximum(m[n], m[n + 1]) * (u[n + 1] - u[n])))
    r02 = c02 * pair_sum(u[0], u[2], s[0], s[2])
    r13 = c02 * pair_sum(u[1], u[3], s[1], s[3])
    r03 = c03 * pair_sum(u[0], u[3], s[0], s[3])
    t0 = -(e[0] + r02 + r03)
    t1 = e[0] - e[1] - r13
    t2 = e[1] - e[2] + r02
    t3 = e[2] + r13 + r03
    return t0, t1, t2, t3


def edge(u, o, cg, cd):
    g = pair_sum(u, o, u * u, o * o)
    return cg * g - cd * (jnp.maximum(jnp.abs(u), jnp.abs(o)) * (u - o))


def rows8(x):
    return jnp.broadcast_to(x, (8, LANES))


def blend_rates(tile_ref, modes_ref, jac_ref, rate_ref):
    n = lax.broadcasted_iota(jnp.int32, (64, LANES), 0)
    top = ((n & 3) == 3) | ((n & 12) == 12) | (n >= 48)
    for g in range(GROUPS):
        cols = slice(g * LANES, (g + 1) * LANES)
        modal = jnp.dot(
            modes_ref[...], tile_ref[g, 0:64, :], precision=lax.Precision.HIGHEST,
            preferred_element_type=F32,
        )
        energy = modal * modal
        high = jnp.sum(jnp.where(top, energy, 0.0), axis=0, keepdims=True)
        full = jnp.sum(energy, axis=0, keepdims=True)
        ratio = high / (full + 1e-06)
        blend = 0.5 * ratio / (ratio + 0.1)
        step = TIME_STEP * jac_ref[0:1, cols]
        rate_ref[0:1, cols] = step * (1.0 - blend)
        rate_ref[1:2, cols] = step * blend
        rate_ref[2:3, cols] = step


def outside_of(source_ref, trace_ref, ghost_ref, ghost_bf, outside_ref):
    for slot in range(4):
        high, rest = split2(ghost_ref[slot])
        ghost_bf[0:80, slot * LANES : (slot + 1) * LANES] = high
        ghost_bf[80:160, slot * LANES : (slot + 1) * LANES] = rest
    for f in range(6):
        index = source_ref[f : f + 1, :]
        far = index - 6 * E_DEV
        slot = (
            (far >= SLOTS).astype(jnp.int32)
            + (far >= 2 * SLOTS).astype(jnp.int32)
            + (far >= 3 * SLOTS).astype(jnp.int32)
        )
        far_row = jnp.where(far >= 0, far + (LANES - SLOTS) * slot, -1)
        near_row = index - (f ^ 1) * E_DEV
        total = jnp.dot(
            trace_ref[f ^ 1], one_hot(near_row, E_DEV, E_DEV), preferred_element_type=F32
        ) + jnp.dot(ghost_bf[...], one_hot(far_row, E_DEV, E_DEV), preferred_element_type=F32)
        outside_ref[f] = total[0:80] + total[80:160]


def update_block(v, g, tile_ref, speed_ref, rate_ref, outside_ref, acc_ref, up_ref):
    base = pl.multiple_of(64 * v, 64)
    face = pl.multiple_of(16 * v, 16)
    cols = pl.ds(pl.multiple_of(g * LANES, LANES), LANES)
    hi = rate_ref[0:1, cols]
    lo = rate_ref[1:2, cols]
    step = rate_ref[2:3, cols]
    low = low_half((8, LANES))

    def coefs(d):
        a = speed_ref[d, v]
        third = (a / 3.0) * hi
        sixth = (a / 6.0) * lo
        return (
            Q01 * third + sixth, Q12 * third + sixth, Q02 * third, Q03 * third,
            (0.5 * jnp.abs(a)) * lo, (a * (END / 6.0)) * step, (0.5 * END) * jnp.abs(a) * step,
        )

    ca, cb, c02, c03, cd, bg, bd = [rows8(c) for c in coefs(0)]
    for h in range(2):
        u = [tile_ref[g, pl.ds(base + 32 * h + i, 8, stride=4), :] for i in range(4)]
        t = line_update(u, (ca, cb, c02, c03, cd))
        ol = outside_ref[0, pl.ds(face + 8 * h, 8), cols]
        orr = outside_ref[1, pl.ds(face + 8 * h, 8), cols]
        acc = [
            END * t[0] + edge(u[0], ol, bg, bd), MID * t[1], MID * t[2],
            END * t[3] + edge(u[3], orr, -bg, bd),
        ]
        for i in range(4):
            acc_ref[pl.ds(32 * h + i, 8, stride=4), :] = acc[i]
    tiles = [tile_ref[g, pl.ds(base + 8 * t, 8), :] for t in range(8)]
    ca, cb, c02, c03, cd, bg, bd = [rows8(c) for c in coefs(2)]
    total = [None] * 8
    for h in range(2):
        u = [tiles[2 * k + h] for k in range(4)]
        t = line_update(u, (ca, cb, c02, c03, cd))
        ol = outside_ref[4, pl.ds(face + 8 * h, 8), cols]
        orr = outside_ref[5, pl.ds(face + 8 * h, 8), cols]
        acc = [
            END * t[0] + edge(u[0], ol, bg, bd), MID * t[1], MID * t[2],
            END * t[3] + edge(u[3], orr, -bg, bd),
        ]
        for k in range(4):
            total[2 * k + h] = acc[k]
    ca, cb, c02, c03, cd, bg, bd = [rows8(c) for c in coefs(1)]
    signed = jnp.where(low, -ca, ca)
    cross = jnp.where(low, -c03, -cb)
    cross_d = jnp.where(low, 0.0, cd)
    wa = jnp.where(low, END, MID)
    wb = jnp.where(low, MID, END)
    bgs = jnp.where(low, bg, -bg)
    outer_l = [outside_ref[2, pl.ds(face + 8 * h, 8), cols] for h in range(2)]
    outer_r = [outside_ref[3, pl.ds(face + 8 * h, 8), cols] for h in range(2)]
    for k in range(4):
        a, b = tiles[2 * k], tiles[2 * k + 1]
        at, bt = turn(a), turn(b)
        sa, sb, sat, sbt = a * a, b * b, at * at, bt * bt
        ma, mb, mat, mbt = jnp.abs(a), jnp.abs(b), jnp.abs(at), jnp.abs(bt)
        x1 = signed * pair_sum(a, at, sa, sat) + cd * (jnp.maximum(ma, mat) * (at - a))
        x2 = signed * pair_sum(b, bt, sb, sbt) + cd * (jnp.maximum(mb, mbt) * (bt - b))
        x3 = c02 * pair_sum(a, b, sa, sb)
        x4 = cross * pair_sum(a, bt, sa, sbt) + cross_d * (jnp.maximum(ma, mbt) * (bt - a))
        ol = outer_l[k // 2]
        orr = outer_r[k // 2]
        outer = jnp.where(low, ol, turn(orr)) if k % 2 == 0 else jnp.where(low, turn(ol), orr)
        bound = edge(jnp.where(low, a, b), outer, bgs, bd)
        total[2 * k] += wa * (x1 - x3 + x4) + jnp.where(low, bound, 0.0)
        total[2 * k + 1] += wb * (x2 + x3 - turn(x4)) + jnp.where(low, 0.0, bound)
    for t in range(8):
        total[t] += tiles[t] + acc_ref[8 * t : 8 * t + 8, :]
    for t in range(4):
        high, rest = split2(jnp.concatenate(total[2 * t : 2 * t + 2], axis=0))
        up_ref[pl.ds(pl.multiple_of(base + 16 * t, 16), 16), cols] = high
        up_ref[pl.ds(pl.multiple_of(ROWS + base + 16 * t, 16), 16), cols] = rest


def refine_tables(flag_ref, jac_ref, start_ref, aux_ref):
    flags = flag_ref[...].astype(F32)
    wide = jnp.broadcast_to(flags, (LANES, E_DEV)).astype(BF16)
    row = lax.broadcasted_iota(jnp.int32, (E_DEV, E_DEV), 0)
    col = lax.broadcasted_iota(jnp.int32, (E_DEV, E_DEV), 1)
    ahead = jnp.where(col < row, 1.0, 0.0).astype(BF16)
    within = jnp.where(col <= row, 1.0, 0.0).astype(BF16)
    dims = (((1,), (1,)), ((), ()))
    place = lax.broadcasted_iota(jnp.int32, (E_DEV, LANES), 0).astype(F32)
    start_ref[0] = place + 7.0 * lax.dot_general(ahead, wide, dims, preferred_element_type=F32)
    start_ref[1] = (
        place + 1.0 + 7.0 * lax.dot_general(within, wide, dims, preferred_element_type=F32)
    )
    count = lax.dot_general(wide[0:16], ahead, dims, preferred_element_type=F32)[0:1]
    at = lax.broadcasted_iota(jnp.int32, (1, E_DEV), 1).astype(F32) + 7.0 * count
    at_high = jnp.floor(at * (1.0 / 16.0))
    jac = jac_ref[...]
    j0, rest = split2(jac)
    rest = jac - j0.astype(F32)
    j1 = rest.astype(BF16)
    j2 = (rest - j1.astype(F32)).astype(BF16)
    zero = jnp.zeros((10, E_DEV), F32)
    aux_ref[...] = jnp.concatenate(
        [
            at_high, at - 16.0 * at_high, flags, j0.astype(F32), j1.astype(F32), j2.astype(F32),
            zero,
        ],
        axis=0,
    ).astype(BF16)


def column_tables(first, before, start_ref, aux_ref, coef_ref, hot_ref):
    lane = lax.broadcasted_iota(jnp.int32, (1, LANES), 1) + first
    place = lane.astype(F32) - 7.0 * before[0:1, :]
    inside = (place >= start_ref[0]) & (place < start_ref[1])
    hot = jnp.where(inside, 1.0, 0.0).astype(BF16)
    hot_ref[...] = hot
    aux = jnp.dot(aux_ref[...], hot, preferred_element_type=F32)
    child = place - (16.0 * aux[0:1] + aux[1:2])
    refined = aux[2:3] > 0.5
    z = child >= 4.0
    child = child - jnp.where(z, 4.0, 0.0)
    y = child >= 2.0
    child = child - jnp.where(y, 2.0, 0.0)
    x = child >= 1.0
    jac = (aux[3:4] + aux[4:5] + aux[5:6]) * jnp.where(refined, 2.0, 1.0)

    def table(bit):
        return [
            [
                rows8(
                    jnp.where(
                        refined,
                        jnp.where(bit, float(SIDES[1][i, m]), float(SIDES[0][i, m])),
                        1.0 if i == m else 0.0,
                    )
                )
                for m in range(4)
            ]
            for i in range(4)
        ]

    cx, cy, cz = table(x), table(y), table(z)
    low = low_half((8, LANES))
    n = 0
    for i in range(4):
        for m in range(4):
            coef_ref[n] = cx[i][m]
            coef_ref[16 + n] = cz[i][m]
            n += 1
    order = [(0, 1), (1, 0), (2, 3), (3, 2)]
    for at, (first_j, last_j) in enumerate(((0, 1), (2, 3))):
        for k, (lo_m, hi_m) in enumerate(order):
            coef_ref[32 + 4 * at + k] = jnp.where(low, cy[first_j][lo_m], cy[last_j][hi_m])
    return jac


def combine4(c, u):
    return (c[0] * u[0] + c[1] * u[1]) + (c[2] * u[2] + c[3] * u[3])


def interpolate(v, pick_ref, coef_ref, line_ref, put):
    base = pl.multiple_of(64 * v, 64)
    tiles = [
        pick_ref[pl.ds(base + 8 * t, 8), :] + pick_ref[pl.ds(ROWS + base + 8 * t, 8), :]
        for t in range(8)
    ]
    mid = [None] * 8
    for h in range(2):
        u = [tiles[2 * k + h] for k in range(4)]
        for k in range(4):
            mid[2 * k + h] = combine4([coef_ref[16 + 4 * k + m] for m in range(4)], u)
    for k in range(4):
        a, b = mid[2 * k], mid[2 * k + 1]
        u = [a, turn(a), b, turn(b)]
        for at in range(2):
            line_ref[16 * k + 8 * at : 16 * k + 8 * at + 8, :] = combine4(
                [coef_ref[32 + 4 * at + m] for m in range(4)], u
            )
    for h in range(2):
        u = [line_ref[pl.ds(32 * h + i, 8, stride=4), :] for i in range(4)]
        for i in range(4):
            put(base + 32 * h + i, combine4([coef_ref[4 * i + m] for m in range(4)], u))


def local_kernel(
    x_ref, jac_ref, speed_ref, flag_ref, source_ref, ghost_ref, before_ref, modes_ref,
    own_ref, own_jac_ref, blocks_ref,
    tile_ref, trace_ref, ghost_bf, outside_ref, rate_ref, acc_ref, up_ref, start_ref, aux_ref, coef_ref,
    hot_ref, pick_ref, line_ref, fetch_sems,
):
    fetches = fetch_state(x_ref, tile_ref, fetch_sems)
    for g in range(GROUPS):
        fetches[g].wait()
        build_traces(tile_ref, trace_ref, g)
    blend_rates(tile_ref, modes_ref, jac_ref, rate_ref)
    outside_of(source_ref, trace_ref, ghost_ref, ghost_bf, outside_ref)

    def step(n, carry):
        update_block(n // GROUPS, n % GROUPS, tile_ref, speed_ref, rate_ref, outside_ref, acc_ref, up_ref)
        return carry

    lax.fori_loop(0, VARS * GROUPS, step, 0)
    refine_tables(flag_ref, jac_ref, start_ref, aux_ref)
    before = before_ref[...]

    def columns(first, put, put_jac):
        put_jac(column_tables(first, before, start_ref, aux_ref, coef_ref, hot_ref))
        pick_ref[...] = jnp.dot(up_ref[...], hot_ref[...], preferred_element_type=F32)

        def one(v, carry):
            interpolate(v, pick_ref, coef_ref, line_ref, put)
            return carry

        lax.fori_loop(0, VARS, one, 0)

    def block_step(n, carry):
        first = jnp.where(n < 2, -2 * LANES + n * LANES, E_NEW + (n - 2) * LANES)
        at = n // 2
        half = n % 2

        def put(row, value):
            blocks_ref[at, half, pl.ds(row, 8, stride=4), :] = value

        def put_jac(value):
            blocks_ref[at, half, ROWS : ROWS + 8, :] = rows8(value)

        columns(first, put, put_jac)
        return carry

    lax.fori_loop(0, 4, block_step, 0)

    def own_step(n, carry):
        first = pl.multiple_of(n * LANES, LANES)
        cols = pl.ds(first, LANES)

        def put(row, value):
            own_ref[n, pl.ds(row, 8, stride=4), :] = value

        def put_jac(value):
            own_jac_ref[0:1, cols] = value

        columns(first, put, put_jac)
        return carry

    lax.fori_loop(0, 8, own_step, 0)


def exchange_kernel(blocks_ref, landed_ref, send_sems, recv_sems):
    me = lax.axis_index("curve")
    devices = ROW_OF * COL_OF
    mates = ((me + devices - 1) % devices, (me + 1) % devices)
    barrier = pltpu.get_barrier_semaphore()
    for mate in mates:
        pl.semaphore_signal(barrier, inc=1, device_id=(mate,), device_id_type=MESH)
    pl.semaphore_wait(barrier, 2)
    copies = []
    for at, mate in enumerate(mates):
        copy = pltpu.make_async_remote_copy(
            src_ref=blocks_ref.at[at], dst_ref=landed_ref.at[at],
            send_sem=send_sems.at[at], recv_sem=recv_sems.at[at],
            device_id=(mate,), device_id_type=MESH,
        )
        copy.start()
        copies.append(copy)
    for copy in copies:
        copy.wait()


def merge_kernel(own_ref, own_jac_ref, landed_ref, out_ref, jac_ref):
    left = lax.broadcasted_iota(jnp.int32, (8, LANES), 1) < LANES // 2

    def rows_of(r, get_own, put):
        own = [get_own(c) for c in range(8)]
        low = [landed_ref[1, c, r, :] for c in range(2)]
        far = [
            pltpu.roll(landed_ref[0, c, r, :], LANES // 2, 1)
            for c in range(2)
        ]
        own[0] += low[0]
        own[1] += low[1]
        own[5] += jnp.where(left, 0.0, far[0])
        own[6] += jnp.where(left, far[0], far[1])
        own[7] += far[1]
        for c in range(8):
            put(c, own[c])

    def step(n, carry):
        r = pl.ds(pl.multiple_of(8 * n, 8), 8)

        def put(c, value):
            if c < 7:
                out_ref[r, c * LANES : (c + 1) * LANES] = value
            else:
                out_ref[r, c * LANES : E_NEW] = value[:, : E_NEW - 7 * LANES]

        rows_of(r, lambda c: own_ref[c, r, :], put)
        return carry

    lax.fori_loop(0, ROWS // 8, step, 0)

    def put_jac(c, value):
        width = min(LANES, E_NEW - c * LANES)
        jac_ref[0:1, c * LANES : c * LANES + width] = value[0:1, :width]

    rows_of(
        pl.ds(ROWS, 8), lambda c: rows8(own_jac_ref[0:1, c * LANES : (c + 1) * LANES]), put_jac
    )


def vmem(count):
    return [pl.BlockSpec(memory_space=pltpu.VMEM)] * count


def shards(nodal_state, inverse_jacobian, speeds, refine_flags, send_index, face_source):
    x = nodal_state.reshape(ROWS, E_DEV)
    jac = inverse_jacobian.reshape(1, E_DEV)
    flags = refine_flags.reshape(1, E_DEV)
    sends = send_index.reshape(1, 4 * SLOTS)
    dma = pltpu.SemaphoreType.DMA
    ghost, before = pl.pallas_call(
        halo_kernel,
        out_shape=(
            jax.ShapeDtypeStruct((4, 80, LANES), F32),
            jax.ShapeDtypeStruct((8, LANES), F32),
        ),
        in_specs=[pl.BlockSpec(memory_space=pl.ANY)] + vmem(2),
        out_specs=tuple(vmem(2)),
        scratch_shapes=[
            pltpu.VMEM((GROUPS, ROWS, LANES), F32),
            pltpu.VMEM((6, 160, E_DEV), BF16),
            pltpu.VMEM((4, 80, LANES), F32),
            pltpu.VMEM((ROW_OF - 1, 1, LANES), F32),
            pltpu.VMEM((COL_OF - 1, 1, LANES), F32),
            pltpu.VMEM((1, LANES), F32),
            pltpu.VMEM((1, LANES), F32),
            dma((GROUPS,)), dma((4,)), dma((4,)), dma((ROW_OF - 1,)), dma((ROW_OF - 1,)),
            dma((COL_OF - 1,)), dma((COL_OF - 1,)),
        ],
        compiler_params=pltpu.CompilerParams(collective_id=0, has_side_effects=True),
        name="halo",
    )(x, sends, flags)
    modes = jnp.asarray(MODES, F32)
    specs = vmem(8)
    specs[0] = pl.BlockSpec(memory_space=pl.ANY)
    specs[2] = pl.BlockSpec(memory_space=pltpu.SMEM)
    own, own_jac, blocks = pl.pallas_call(
        local_kernel,
        out_shape=(
            jax.ShapeDtypeStruct((8, ROWS, LANES), F32),
            jax.ShapeDtypeStruct((1, 1024), F32),
            jax.ShapeDtypeStruct((2, 2, ROWS + 8, LANES), F32),
        ),
        in_specs=specs,
        out_specs=tuple(vmem(3)),
        scratch_shapes=[
            pltpu.VMEM((GROUPS, ROWS, LANES), F32),
            pltpu.VMEM((6, 160, E_DEV), BF16),
            pltpu.VMEM((160, E_DEV), BF16),
            pltpu.VMEM((6, 80, E_DEV), F32),
            pltpu.VMEM((8, E_DEV), F32),
            pltpu.VMEM((64, LANES), F32),
            pltpu.VMEM((2 * ROWS, E_DEV), BF16),
            pltpu.VMEM((2, E_DEV, LANES), F32),
            pltpu.VMEM((16, E_DEV), BF16),
            pltpu.VMEM((40, 8, LANES), F32),
            pltpu.VMEM((E_DEV, LANES), BF16),
            pltpu.VMEM((2 * ROWS, LANES), F32),
            pltpu.VMEM((64, LANES), F32),
            dma((GROUPS,)),
        ],
        name="local",
    )(x, jac, speeds, flags, face_source, ghost, before, modes)
    landed = pl.pallas_call(
        exchange_kernel,
        out_shape=jax.ShapeDtypeStruct((2, 2, ROWS + 8, LANES), F32),
        in_specs=vmem(1),
        out_specs=vmem(1)[0],
        scratch_shapes=[dma((2,)), dma((2,))],
        compiler_params=pltpu.CompilerParams(collective_id=1, has_side_effects=True),
        name="exchange",
    )(blocks)
    out, out_jac = pl.pallas_call(
        merge_kernel,
        out_shape=(
            jax.ShapeDtypeStruct((ROWS, E_NEW), F32),
            jax.ShapeDtypeStruct((1, E_NEW), F32),
        ),
        in_specs=vmem(3),
        out_specs=tuple(vmem(2)),
        name="merge",
    )(own, own_jac, landed)
    return out.reshape(VARS, 64, E_NEW), out_jac.reshape(E_NEW)


def solution(mesh):
    axis = P("curve")
    wide = P(None, None, "curve")
    return jax.shard_map(
        shards,
        mesh=mesh,
        in_specs=(wide, axis, P(), axis, axis, P(None, "curve")),
        out_specs=(wide, axis),
        check_vma=False,
    )
```

profile of v0, /device:TPU:0, one launch (start us, length us, event | category | flops | bytes accessed | tf_op | source)
XLA Modules:
  0.0 53.2 jit_solution(11125047795520147878)
XLA Ops:
  0.6 1.2 %reshape.25.send_ref = s32[1,384]{1,0:T(1,128)} reshape(s32[384]{0:T(512)} %param.11) | data formatting | bytes 3072 | tf_op jit(solution)/shard_map/reshape | solution.py:590
  1.9 17.3 %halo.1 = (f32[4,80,128]{2,1,0:T(8,128)}, f32[8,128]{1,0:T(8,128)}) custom-call(f32[320,512]{1,0:T(8,128)} %bitcast.5, s32[1,384]{1,0:T(1,128)} %reshape.25.send_ref, s32[1,512]{1,0:T(1,128)} %bitcast.7), custom_call_target="tpu_custom_call" | custom-call | tf_op jit(solution)/shard_map/halo/pallas_call | solution.py:592
  19.2 14.4 %local.1 = (f32[8,320,128]{2,1,0:T(8,128)}, f32[1,1024]{1,0:T(1,128)}, f32[2,2,328,128]{3,2,1,0:T(8,128)}) custom-call(f32[320,512]{1,0:T(8,128)} %bitcast.6, f32[1,512]{1,0:T(1,128)} %bitcast.9, f32[3,5]{1,0:T(4,128)} %speed_ref.1, s32[1,512]{1,0:T(1,128)} %bitcast.8, s32[6,512]{1,0:T(8,128)} %source_ref.1, f32[4,80,128]{2,1,0:T(8,128)} %get-tuple-element.9.ghost_ref, ...), custom_call_target="tpu_custom_call" | custom-call | tf_op jit(solution)/shard_map/local/pallas_call | solution.py:618
  33.6 14.1 %exchange.1.landed_ref = f32[2,2,328,128]{3,2,1,0:T(8,128)} custom-call(f32[2,2,328,128]{3,2,1,0:T(8,128)} %get-tuple-element.13.blocks_ref), custom_call_target="tpu_custom_call" | custom-call | tf_op jit(solution)/shard_map/exchange/pallas_call | solution.py:645
  47.7 5.5 %merge.1 = (f32[320,960]{1,0:T(8,128)}, f32[1,960]{1,0:T(1,128)}) custom-call(f32[8,320,128]{2,1,0:T(8,128)} %get-tuple-element.11.own_ref, f32[1,1024]{1,0:T(1,128)} %get-tuple-element.12.own_jac_ref, f32[2,2,328,128]{3,2,1,0:T(8,128)} %exchange.1.landed_ref), custom_call_target="tpu_custom_call" | custom-call | tf_op jit(solution)/shard_map/merge/pallas_call | solution.py:654
where the time goes:
time: 53.5 us; the launch traced here: 53.2 us
  Pallas kernels  51.3 us (96%)
  local copies, waits for them, and re-layouts  1.25 us (2%)
  between operations  0.65 us (1%)
    pallas_call x1, Pallas kernels, shards(): pl.pallas_call(halo_kernel, out_shape=(jax.ShapeDtypeStruct((4, 80, LANES...  17.3 us
    pallas_call x1, Pallas kernels, shards(): pl.pallas_call(local_kernel, out_shape=(jax.ShapeDtypeStruct((8, ROWS, LA...  14.4 us
    pallas_call x1, Pallas kernels, shards(): pl.pallas_call(exchange_kernel, out_shape=jax.ShapeDtypeStruct((2, 2, ROW...  14.1 us
    pallas_call x1, Pallas kernels, shards(): pl.pallas_call(merge_kernel, out_shape=(jax.ShapeDtypeStruct((ROWS, E_NEW...  5.46 us
    reshape x1, local copies, waits for them, and re-layouts, shards(): sends = send_index.reshape(1, 4 * SLOTS)  1.25 us

commit v1 on v0

v1 whole, which is shorter than its diff:
```python
import functools
import math

import jax
import jax.numpy as jnp
import numpy as np
from jax import lax
from jax.experimental import pallas as pl
from jax.experimental.pallas import tpu as pltpu
from jax.sharding import PartitionSpec as P

TIME_STEP = 0.02
VARS = 5
E_DEV = 512
E_NEW = 960
SLOTS = 96
ROWS = 64 * VARS
LANES = 128
GROUPS = E_DEV // LANES
ROW_OF = 8
COL_OF = 16
F32 = jnp.float32
BF16 = jnp.bfloat16
MESH = pl.DeviceIdType.MESH


def lagrange_at(points, targets):
    values_at = np.ones((len(targets), 4))
    for basis_id in range(4):
        for partner in range(4):
            if partner != basis_id:
                values_at[:, basis_id] *= (targets - points[partner]) / (
                    points[basis_id] - points[partner]
                )
    return values_at


def tables():
    root = 1.0 / math.sqrt(5.0)
    points = np.array([-1.0, -root, root, 1.0])
    weights = np.array([1.0, 5.0, 5.0, 1.0]) / 6.0
    bary = np.ones(4)
    for a in range(4):
        for b in range(4):
            if a != b:
                bary[a] /= points[a] - points[b]
    deriv = np.zeros((4, 4))
    for a in range(4):
        for b in range(4):
            if a != b:
                deriv[a, b] = bary[b] / bary[a] / (points[a] - points[b])
        deriv[a, a] = -np.sum(deriv[a])
    skew = weights[:, None] * deriv
    legendre = np.stack(
        [points**0, points, 0.5 * (3 * points**2 - 1), 0.5 * (5 * points**3 - 3 * points)], axis=1
    )
    to_modes = np.linalg.inv(legendre)
    sides = [lagrange_at(points, (points - 1.0) / 2.0), lagrange_at(points, (points + 1.0) / 2.0)]
    return skew, np.kron(to_modes, np.kron(to_modes, to_modes)), sides


SKEW, MODES, SIDES = tables()
Q01, Q02, Q03, Q12 = (float(SKEW[0, 1]), float(SKEW[0, 2]), float(SKEW[0, 3]), float(SKEW[1, 2]))
END, MID = 6.0, 1.2


def split2(x):
    high = x.astype(BF16)
    return high, (x - high.astype(F32)).astype(BF16)


def low_half(shape):
    return (lax.broadcasted_iota(jnp.int32, shape, 0) & 7) < 4


def turn(x):
    return pltpu.roll(x, 4, 0)


def fetch_state(x_ref, tile_ref, sems):
    copies = []
    for g in range(GROUPS):
        copy = pltpu.make_async_copy(
            x_ref.at[:, g * LANES : (g + 1) * LANES], tile_ref.at[g], sems.at[g]
        )
        copy.start()
        copies.append(copy)
    return copies


def build_traces(tile_ref, trace_ref, g):
    low = low_half((8, LANES))
    cols = slice(g * LANES, (g + 1) * LANES)
    for v in range(VARS):
        base = 64 * v
        tiles = [tile_ref[g, base + 8 * t : base + 8 * t + 8, :] for t in range(8)]
        first, last = tiles[0::2], tiles[1::2]
        sets = {
            0: [tile_ref[g, pl.ds(base + 32 * h, 8, stride=4), :] for h in range(2)],
            1: [tile_ref[g, pl.ds(base + 32 * h + 3, 8, stride=4), :] for h in range(2)],
            2: [jnp.where(low, first[k], turn(first[k + 1])) for k in (0, 2)],
            3: [jnp.where(low, turn(last[k]), last[k + 1]) for k in (0, 2)],
            4: tiles[0:2],
            5: tiles[6:8],
        }
        for f, rows in sets.items():
            high, rest = split2(jnp.concatenate(rows, axis=0))
            trace_ref[f, 16 * v : 16 * v + 16, cols] = high
            trace_ref[f, 80 + 16 * v : 96 + 16 * v, cols] = rest


def one_hot(index, size, width):
    rows = lax.broadcasted_iota(jnp.int32, (size, width), 0)
    return jnp.where(rows == index, 1.0, 0.0).astype(BF16)


def gather_sends(send_ref, trace_ref, out_ref):
    packed = jnp.broadcast_to(send_ref[...].reshape(1, 4 * SLOTS), (8, 4 * SLOTS))
    for block in range(4):
        shift = (4 * SLOTS - SLOTS * block) % (4 * SLOTS)
        moved = packed if shift == 0 else pltpu.roll(packed, shift, 1)
        index = moved[0:1, 0:LANES]
        total = jnp.zeros((160, LANES), F32)
        for f in range(6):
            total = total + jnp.dot(
                trace_ref[f],
                one_hot(index - f * E_DEV, E_DEV, LANES),
                preferred_element_type=F32,
            )
        out_ref[block] = total[0:80] + total[80:160]


def pair_sum(ui, um, si, sm):
    return (si + sm) + ui * um


def line_update(u, coef):
    ca, cb, c02, c03, cd = coef
    s = [x * x for x in u]
    m = [jnp.abs(x) for x in u]
    e = []
    for n, c in ((0, ca), (1, cb), (2, ca)):
        g = pair_sum(u[n], u[n + 1], s[n], s[n + 1])
        e.append(c * g - cd * (jnp.maximum(m[n], m[n + 1]) * (u[n + 1] - u[n])))
    r02 = c02 * pair_sum(u[0], u[2], s[0], s[2])
    r13 = c02 * pair_sum(u[1], u[3], s[1], s[3])
    r03 = c03 * pair_sum(u[0], u[3], s[0], s[3])
    t0 = -(e[0] + r02 + r03)
    t1 = e[0] - e[1] - r13
    t2 = e[1] - e[2] + r02
    t3 = e[2] + r13 + r03
    return t0, t1, t2, t3


def edge(u, o, cg, cd):
    g = pair_sum(u, o, u * u, o * o)
    return cg * g - cd * (jnp.maximum(jnp.abs(u), jnp.abs(o)) * (u - o))


def rows8(x):
    return jnp.broadcast_to(x, (8, LANES))


def blend_rates(tile_ref, modes_ref, jac_ref, rate_ref):
    n = lax.broadcasted_iota(jnp.int32, (64, LANES), 0)
    top = ((n & 3) == 3) | ((n & 12) == 12) | (n >= 48)
    for g in range(GROUPS):
        cols = slice(g * LANES, (g + 1) * LANES)
        modal = jnp.dot(
            modes_ref[...], tile_ref[g, 0:64, :], precision=lax.Precision.HIGHEST,
            preferred_element_type=F32,
        )
        energy = modal * modal
        high = jnp.sum(jnp.where(top, energy, 0.0), axis=0, keepdims=True)
        full = jnp.sum(energy, axis=0, keepdims=True)
        ratio = high / (full + 1e-06)
        blend = 0.5 * ratio / (ratio + 0.1)
        step = TIME_STEP * jac_ref[0:1, cols]
        rate_ref[0:1, cols] = step * (1.0 - blend)
        rate_ref[1:2, cols] = step * blend
        rate_ref[2:3, cols] = step


def outside_near(source_ref, trace_ref, outside_ref):
    for f in range(6):
        near_row = source_ref[f : f + 1, :] - (f ^ 1) * E_DEV
        total = jnp.dot(
            trace_ref[f ^ 1], one_hot(near_row, E_DEV, E_DEV), preferred_element_type=F32
        )
        outside_ref[f] = total[0:80] + total[80:160]


def outside_far(source_ref, ghost_ref, ghost_bf, outside_ref):
    for slot in range(4):
        high, rest = split2(ghost_ref[slot])
        ghost_bf[0:80, slot * LANES : (slot + 1) * LANES] = high
        ghost_bf[80:160, slot * LANES : (slot + 1) * LANES] = rest
    for f in range(6):
        far = source_ref[f : f + 1, :] - 6 * E_DEV
        slot = (
            (far >= SLOTS).astype(jnp.int32)
            + (far >= 2 * SLOTS).astype(jnp.int32)
            + (far >= 3 * SLOTS).astype(jnp.int32)
        )
        far_row = jnp.where(far >= 0, far + (LANES - SLOTS) * slot, -1)
        total = jnp.dot(ghost_bf[...], one_hot(far_row, E_DEV, E_DEV), preferred_element_type=F32)
        outside_ref[f] += total[0:80] + total[80:160]


def coefs_of(d, v, speed_ref, hi, lo):
    a = speed_ref[d, v]
    third = (a / 3.0) * hi
    sixth = (a / 6.0) * lo
    return [
        rows8(c)
        for c in (
            Q01 * third + sixth, Q12 * third + sixth, Q02 * third, Q03 * third,
            (0.5 * jnp.abs(a)) * lo,
        )
    ]


def interior_block(v, g, tile_ref, speed_ref, rate_ref, state_ref):
    base = pl.multiple_of(64 * v, 64)
    cols = pl.ds(pl.multiple_of(g * LANES, LANES), LANES)
    hi = rate_ref[0:1, cols]
    lo = rate_ref[1:2, cols]
    low = low_half((8, LANES))
    coef = coefs_of(0, v, speed_ref, hi, lo)
    for h in range(2):
        u = [tile_ref[g, pl.ds(base + 32 * h + i, 8, stride=4), :] for i in range(4)]
        t = line_update(u, coef)
        for i, w in enumerate((END, MID, MID, END)):
            state_ref[g, pl.ds(base + 32 * h + i, 8, stride=4), :] = u[i] + w * t[i]
    tiles = [tile_ref[g, pl.ds(base + 8 * t, 8), :] for t in range(8)]
    coef = coefs_of(2, v, speed_ref, hi, lo)
    total = [None] * 8
    for h in range(2):
        t = line_update([tiles[2 * k + h] for k in range(4)], coef)
        for k, w in enumerate((END, MID, MID, END)):
            total[2 * k + h] = w * t[k]
    ca, cb, c02, c03, cd = coefs_of(1, v, speed_ref, hi, lo)
    signed = jnp.where(low, -ca, ca)
    cross = jnp.where(low, -c03, -cb)
    cross_d = jnp.where(low, 0.0, cd)
    wa = jnp.where(low, END, MID)
    wb = jnp.where(low, MID, END)
    for k in range(4):
        a, b = tiles[2 * k], tiles[2 * k + 1]
        at, bt = turn(a), turn(b)
        sa, sb, sat, sbt = a * a, b * b, at * at, bt * bt
        ma, mb, mat, mbt = jnp.abs(a), jnp.abs(b), jnp.abs(at), jnp.abs(bt)
        x1 = signed * pair_sum(a, at, sa, sat) + cd * (jnp.maximum(ma, mat) * (at - a))
        x2 = signed * pair_sum(b, bt, sb, sbt) + cd * (jnp.maximum(mb, mbt) * (bt - b))
        x3 = c02 * pair_sum(a, b, sa, sb)
        x4 = cross * pair_sum(a, bt, sa, sbt) + cross_d * (jnp.maximum(ma, mbt) * (bt - a))
        total[2 * k] += wa * (x1 - x3 + x4)
        total[2 * k + 1] += wb * (x2 + x3 - turn(x4))
    for t in range(8):
        state_ref[g, pl.ds(base + 8 * t, 8), :] += total[t]


def edge_block(v, g, tile_ref, speed_ref, rate_ref, outside_ref, state_ref, up_ref):
    base = pl.multiple_of(64 * v, 64)
    face = pl.multiple_of(16 * v, 16)
    cols = pl.ds(pl.multiple_of(g * LANES, LANES), LANES)
    step = rate_ref[2:3, cols]
    low = low_half((8, LANES))

    def coefs(d):
        a = speed_ref[d, v]
        return rows8((a * (END / 6.0)) * step), rows8((0.5 * END) * jnp.abs(a) * step)

    bg, bd = coefs(0)
    for h in range(2):
        for f, i, sign in ((0, 0, bg), (1, 3, -bg)):
            rows = pl.ds(base + 32 * h + i, 8, stride=4)
            outer = outside_ref[f, pl.ds(face + 8 * h, 8), cols]
            state_ref[g, rows, :] += edge(tile_ref[g, rows, :], outer, sign, bd)
    tiles = [tile_ref[g, pl.ds(base + 8 * t, 8), :] for t in range(8)]
    total = [state_ref[g, pl.ds(base + 8 * t, 8), :] for t in range(8)]
    bg, bd = coefs(2)
    for h in range(2):
        for f, k, sign in ((4, 0, bg), (5, 3, -bg)):
            outer = outside_ref[f, pl.ds(face + 8 * h, 8), cols]
            total[2 * k + h] += edge(tiles[2 * k + h], outer, sign, bd)
    bg, bd = coefs(1)
    bgs = jnp.where(low, bg, -bg)
    outer_l = [outside_ref[2, pl.ds(face + 8 * h, 8), cols] for h in range(2)]
    outer_r = [outside_ref[3, pl.ds(face + 8 * h, 8), cols] for h in range(2)]
    for k in range(4):
        ol = outer_l[k // 2]
        orr = outer_r[k // 2]
        outer = jnp.where(low, ol, turn(orr)) if k % 2 == 0 else jnp.where(low, turn(ol), orr)
        bound = edge(jnp.where(low, tiles[2 * k], tiles[2 * k + 1]), outer, bgs, bd)
        total[2 * k] += jnp.where(low, bound, 0.0)
        total[2 * k + 1] += jnp.where(low, 0.0, bound)
    for t in range(4):
        high, rest = split2(jnp.concatenate(total[2 * t : 2 * t + 2], axis=0))
        up_ref[pl.ds(pl.multiple_of(base + 16 * t, 16), 16), cols] = high
        up_ref[pl.ds(pl.multiple_of(ROWS + base + 16 * t, 16), 16), cols] = rest


def refine_tables(flag_ref, jac_ref, start_ref, aux_ref):
    flags = flag_ref[...].astype(F32)
    wide = jnp.broadcast_to(flags, (LANES, E_DEV)).astype(BF16)
    row = lax.broadcasted_iota(jnp.int32, (E_DEV, E_DEV), 0)
    col = lax.broadcasted_iota(jnp.int32, (E_DEV, E_DEV), 1)
    ahead = jnp.where(col < row, 1.0, 0.0).astype(BF16)
    within = jnp.where(col <= row, 1.0, 0.0).astype(BF16)
    dims = (((1,), (1,)), ((), ()))
    place = lax.broadcasted_iota(jnp.int32, (E_DEV, LANES), 0).astype(F32)
    start_ref[0] = place + 7.0 * lax.dot_general(ahead, wide, dims, preferred_element_type=F32)
    start_ref[1] = (
        place + 1.0 + 7.0 * lax.dot_general(within, wide, dims, preferred_element_type=F32)
    )
    count = lax.dot_general(wide[0:16], ahead, dims, preferred_element_type=F32)[0:1]
    at = lax.broadcasted_iota(jnp.int32, (1, E_DEV), 1).astype(F32) + 7.0 * count
    at_high = jnp.floor(at * (1.0 / 16.0))
    jac = jac_ref[...]
    j0, rest = split2(jac)
    rest = jac - j0.astype(F32)
    j1 = rest.astype(BF16)
    j2 = (rest - j1.astype(F32)).astype(BF16)
    zero = jnp.zeros((10, E_DEV), F32)
    aux_ref[...] = jnp.concatenate(
        [
            at_high, at - 16.0 * at_high, flags, j0.astype(F32), j1.astype(F32), j2.astype(F32),
            zero,
        ],
        axis=0,
    ).astype(BF16)


def column_tables(tile, first, before, start_ref, aux_ref, coef_ref, hot_ref):
    lane = lax.broadcasted_iota(jnp.int32, (1, LANES), 1) + first
    place = lane.astype(F32) - 7.0 * before[0:1, :]
    inside = (place >= start_ref[0]) & (place < start_ref[1])
    hot = jnp.where(inside, 1.0, 0.0).astype(BF16)
    cols = pl.ds(pl.multiple_of((tile % 2) * LANES, LANES), LANES)
    hot_ref[tile // 2, :, cols] = hot
    aux = jnp.dot(aux_ref[...], hot, preferred_element_type=F32)
    child = place - (16.0 * aux[0:1] + aux[1:2])
    refined = aux[2:3] > 0.5
    z = child >= 4.0
    child = child - jnp.where(z, 4.0, 0.0)
    y = child >= 2.0
    child = child - jnp.where(y, 2.0, 0.0)
    x = child >= 1.0
    jac = (aux[3:4] + aux[4:5] + aux[5:6]) * jnp.where(refined, 2.0, 1.0)

    def table(bit):
        return [
            [
                rows8(
                    jnp.where(
                        refined,
                        jnp.where(bit, float(SIDES[1][i, m]), float(SIDES[0][i, m])),
                        1.0 if i == m else 0.0,
                    )
                )
                for m in range(4)
            ]
            for i in range(4)
        ]

    cx, cy, cz = table(x), table(y), table(z)
    low = low_half((8, LANES))
    n = 0
    for i in range(4):
        for m in range(4):
            coef_ref[tile, n] = cx[i][m]
            coef_ref[tile, 16 + n] = cz[i][m]
            n += 1
    order = [(0, 1), (1, 0), (2, 3), (3, 2)]
    for at, (first_j, last_j) in enumerate(((0, 1), (2, 3))):
        for k, (lo_m, hi_m) in enumerate(order):
            coef_ref[tile, 32 + 4 * at + k] = jnp.where(low, cy[first_j][lo_m], cy[last_j][hi_m])
    return jac


def combine4(c, u):
    return (c[0] * u[0] + c[1] * u[1]) + (c[2] * u[2] + c[3] * u[3])


def interpolate(v, tile, half, pick_ref, coef_ref, line_ref, put):
    base = pl.multiple_of(64 * v, 64)
    cols = slice(half * LANES, half * LANES + LANES)
    tiles = [
        pick_ref[pl.ds(base + 8 * t, 8), cols] + pick_ref[pl.ds(ROWS + base + 8 * t, 8), cols]
        for t in range(8)
    ]
    mid = [None] * 8
    for h in range(2):
        u = [tiles[2 * k + h] for k in range(4)]
        for k in range(4):
            mid[2 * k + h] = combine4([coef_ref[tile, 16 + 4 * k + m] for m in range(4)], u)
    for k in range(4):
        a, b = mid[2 * k], mid[2 * k + 1]
        u = [a, turn(a), b, turn(b)]
        for at in range(2):
            line_ref[16 * k + 8 * at : 16 * k + 8 * at + 8, :] = combine4(
                [coef_ref[tile, 32 + 4 * at + m] for m in range(4)], u
            )
    for h in range(2):
        u = [line_ref[pl.ds(32 * h + i, 8, stride=4), :] for i in range(4)]
        for i in range(4):
            put(base + 32 * h + i, combine4([coef_ref[tile, 4 * i + m] for m in range(4)], u))


def merge(own_ref, own_jac_ref, landed_ref, out_ref, jac_ref):
    left = lax.broadcasted_iota(jnp.int32, (8, LANES), 1) < LANES // 2

    def rows_of(r, own, put):
        low = [landed_ref[1, c, r, :] for c in range(2)]
        far = [pltpu.roll(landed_ref[0, c, r, :], LANES // 2, 1) for c in range(2)]
        own[0] += low[0]
        own[1] += low[1]
        own[5] += jnp.where(left, 0.0, far[0])
        own[6] += jnp.where(left, far[0], far[1])
        own[7] += far[1]
        for c in range(8):
            put(c, own[c])

    def step(n, carry):
        r = pl.ds(pl.multiple_of(8 * n, 8), 8)

        def put(c, value):
            if c < 7:
                out_ref[r, c * LANES : (c + 1) * LANES] = value
            else:
                out_ref[r, c * LANES : E_NEW] = value[:, : E_NEW - 7 * LANES]

        rows_of(r, [own_ref[c, r, :] for c in range(8)], put)
        return carry

    lax.fori_loop(0, ROWS // 8, step, 0, unroll=4)

    def put_jac(c, value):
        width = min(LANES, E_NEW - c * LANES)
        jac_ref[0:1, c * LANES : c * LANES + width] = value[0:1, :width]

    rows_of(pl.ds(ROWS, 8), [own_jac_ref[c] for c in range(8)], put_jac)


def kernel(
    x_ref, jac_ref, speed_ref, flag_ref, send_ref, source_ref, modes_ref,
    out_ref, out_jac_ref,
    tile_ref, trace_ref, out_buf, ghost_ref, ghost_bf, outside_ref, rate_ref, state_ref, up_ref,
    start_ref, aux_ref, coef_ref, hot_ref, pick_ref, line_ref, own_ref, own_jac_ref,
    blocks_ref, landed_ref, row_buf, col_buf, mine, group,
    fetch_sems, send_sems, recv_sems, row_send, row_recv, col_send, col_recv,
    block_send, block_recv,
):
    me = lax.axis_index("curve")
    devices = ROW_OF * COL_OF
    row_at = me % ROW_OF
    col_at = me // ROW_OF
    near = [(me + devices + o) % devices for o in (-2, -1, 1, 2)]
    row_mates = [col_at * ROW_OF + (row_at + k) % ROW_OF for k in range(1, ROW_OF)]
    col_mates = [((col_at + k) % COL_OF) * ROW_OF + row_at for k in range(1, COL_OF)]
    partners = near + row_mates + col_mates
    barrier = pltpu.get_barrier_semaphore()
    for partner in partners:
        pl.semaphore_signal(barrier, inc=1, device_id=(partner,), device_id_type=MESH)
    fetches = fetch_state(x_ref, tile_ref, fetch_sems)

    def send(src, dst, send_sem, recv_sem, mate):
        copy = pltpu.make_async_remote_copy(
            src_ref=src, dst_ref=dst, send_sem=send_sem, recv_sem=recv_sem,
            device_id=(mate,), device_id_type=MESH,
        )
        copy.start()
        return copy

    count = jnp.sum(flag_ref[...].astype(F32), axis=1, keepdims=True)
    mine[...] = jnp.broadcast_to(count - 64.0, (1, LANES))
    for g in range(GROUPS):
        fetches[g].wait()
        build_traces(tile_ref, trace_ref, g)
    gather_sends(send_ref, trace_ref, out_buf)
    pl.semaphore_wait(barrier, len(partners))
    row_copies = [
        send(mine, row_buf.at[k], row_send.at[k], row_recv.at[k], mate)
        for k, mate in enumerate(row_mates)
    ]
    halo = [
        send(out_buf.at[b], ghost_ref.at[3 - b], send_sems.at[b], recv_sems.at[3 - b], mate)
        for b, mate in enumerate(near)
    ]
    outside_near(source_ref, trace_ref, outside_ref)
    blend_rates(tile_ref, modes_ref, jac_ref, rate_ref)
    for copy in row_copies:
        copy.wait()
    total = mine[...]
    behind = jnp.zeros((1, LANES), F32)
    for k in range(ROW_OF - 1):
        value = row_buf[k]
        total = total + value
        behind = behind + jnp.where(row_at >= k + 1, value, 0.0)
    group[...] = total
    col_copies = [
        send(group, col_buf.at[k], col_send.at[k], col_recv.at[k], mate)
        for k, mate in enumerate(col_mates)
    ]

    def interior_step(n, carry):
        interior_block(n // GROUPS, n % GROUPS, tile_ref, speed_ref, rate_ref, state_ref)
        return carry

    lax.fori_loop(0, VARS * GROUPS, interior_step, 0)
    refine_tables(flag_ref, jac_ref, start_ref, aux_ref)
    for b in range(4):
        halo[b].wait_send()
        halo[3 - b].wait_recv()
    outside_far(source_ref, ghost_ref, ghost_bf, outside_ref)

    def edge_step(n, carry):
        edge_block(
            n // GROUPS, n % GROUPS, tile_ref, speed_ref, rate_ref, outside_ref, state_ref, up_ref
        )
        return carry

    lax.fori_loop(0, VARS * GROUPS, edge_step, 0)
    for copy in col_copies:
        copy.wait()
    for k in range(COL_OF - 1):
        behind = behind + jnp.where(col_at >= k + 1, col_buf[k], 0.0)

    def table(tile, first):
        return rows8(
            column_tables(tile, first, behind, start_ref, aux_ref, coef_ref, hot_ref)
        )

    def pick(pair):
        pick_ref[...] = jnp.dot(up_ref[...], hot_ref[pair], preferred_element_type=F32)

    blocks = []
    for at, first in enumerate((-2 * LANES, E_NEW)):
        for half in range(2):
            blocks_ref[at, half, ROWS : ROWS + 8, :] = table(2 * at + half, first + half * LANES)
        pick(at)
        for half in range(2):

            def block_step(v, carry, at=at, half=half):
                def put(row, value):
                    blocks_ref[at, half, pl.ds(row, 8, stride=4), :] = value

                interpolate(v, 2 * at + half, half, pick_ref, coef_ref, line_ref, put)
                return carry

            lax.fori_loop(0, VARS, block_step, 0)
            blocks.append(
                send(
                    blocks_ref.at[at, half], landed_ref.at[at, half],
                    block_send.at[2 * at + half], block_recv.at[2 * at + half], near[1 + at],
                )
            )

    def own_step(pair, carry):
        for half in range(2):
            c = 2 * pair + half
            own_jac_ref[c] = table(c + 4, c * LANES)
        pick(pair + 2)
        for half in range(2):

            def one(v, carry, half=half):
                def put(row, value):
                    own_ref[2 * pair + half, pl.ds(row, 8, stride=4), :] = value

                interpolate(v, 2 * pair + half + 4, half, pick_ref, coef_ref, line_ref, put)
                return carry

            lax.fori_loop(0, VARS, one, 0)
        return carry

    lax.fori_loop(0, 4, own_step, 0)
    for copy in blocks:
        copy.wait()
    merge(own_ref, own_jac_ref, landed_ref, out_ref, out_jac_ref)


def vmem(count):
    return [pl.BlockSpec(memory_space=pltpu.VMEM)] * count


def shards(nodal_state, inverse_jacobian, speeds, refine_flags, send_index, face_source):
    x = nodal_state.reshape(ROWS, E_DEV)
    jac = inverse_jacobian.reshape(1, E_DEV)
    flags = refine_flags.reshape(1, E_DEV)
    dma = pltpu.SemaphoreType.DMA
    specs = vmem(7)
    specs[0] = pl.BlockSpec(memory_space=pl.ANY)
    specs[2] = pl.BlockSpec(memory_space=pltpu.SMEM)
    out, out_jac = pl.pallas_call(
        kernel,
        out_shape=(
            jax.ShapeDtypeStruct((ROWS, E_NEW), F32),
            jax.ShapeDtypeStruct((1, E_NEW), F32),
        ),
        in_specs=specs,
        out_specs=tuple(vmem(2)),
        scratch_shapes=[
            pltpu.VMEM((GROUPS, ROWS, LANES), F32),
            pltpu.VMEM((6, 160, E_DEV), BF16),
            pltpu.VMEM((4, 80, LANES), F32),
            pltpu.VMEM((4, 80, LANES), F32),
            pltpu.VMEM((160, E_DEV), BF16),
            pltpu.VMEM((6, 80, E_DEV), F32),
            pltpu.VMEM((8, E_DEV), F32),
            pltpu.VMEM((GROUPS, ROWS, LANES), F32),
            pltpu.VMEM((2 * ROWS, E_DEV), BF16),
            pltpu.VMEM((2, E_DEV, LANES), F32),
            pltpu.VMEM((16, E_DEV), BF16),
            pltpu.VMEM((12, 40, 8, LANES), F32),
            pltpu.VMEM((6, E_DEV, 2 * LANES), BF16),
            pltpu.VMEM((2 * ROWS, 2 * LANES), F32),
            pltpu.VMEM((64, LANES), F32),
            pltpu.VMEM((8, ROWS, LANES), F32),
            pltpu.VMEM((8, 8, LANES), F32),
            pltpu.VMEM((2, 2, ROWS + 8, LANES), F32),
            pltpu.VMEM((2, 2, ROWS + 8, LANES), F32),
            pltpu.VMEM((ROW_OF - 1, 1, LANES), F32),
            pltpu.VMEM((COL_OF - 1, 1, LANES), F32),
            pltpu.VMEM((1, LANES), F32),
            pltpu.VMEM((1, LANES), F32),
            dma((GROUPS,)), dma((4,)), dma((4,)), dma((ROW_OF - 1,)), dma((ROW_OF - 1,)),
            dma((COL_OF - 1,)), dma((COL_OF - 1,)), dma((4,)), dma((4,)),
        ],
        compiler_params=pltpu.CompilerParams(collective_id=0, has_side_effects=True),
        name="step",
    )(x, jac, speeds, flags, send_index, face_source, jnp.asarray(MODES, F32))
    return out.reshape(VARS, 64, E_NEW), out_jac.reshape(E_NEW)


def solution(mesh):
    axis = P("curve")
    wide = P(None, None, "curve")
    return jax.shard_map(
        shards,
        mesh=mesh,
        in_specs=(wide, axis, P(), axis, axis, P(None, "curve")),
        out_specs=(wide, axis),
        check_vma=False,
    )
```

time: 53.5 us -> 33.9 us (0.63)
  Pallas kernels: 51.3 us -> 29.9 us
  local copies, waits for them, and re-layouts: 1.25 us -> 3.12 us
    pallas_call x4 -> x1, Pallas kernels: 51.3 us -> 29.9 us  [shards(): pl.pallas_call(kernel, out_shape=(jax.ShapeDtypeStruct((ROWS, E_NEW), F32...]
    unnamed x0 -> x4, local copies, waits for them, and re-layouts: none -> 3.12 us
    reshape x1 -> x0, local copies, waits for them, and re-layouts: 1.25 us -> none  [shards(): sends = send_index.reshape(1, 4 * SLOTS)]
where the time goes in v1:
time: 33.9 us; the launch traced here: 33.7 us
  Pallas kernels  29.9 us (88%)
  local copies, waits for them, and re-layouts  3.12 us (9%)
  between operations  0.65 us (2%)
    pallas_call x1, Pallas kernels, shards(): pl.pallas_call(kernel, out_shape=(jax.ShapeDtypeStruct((ROWS, E_NEW), F32...  29.9 us
    unnamed x4, local copies, waits for them, and re-layouts  3.12 us

profile of v1, /device:TPU:0, one launch (start us, length us, event | category | flops | bytes accessed | tf_op | source)
XLA Modules:
  0.0 33.7 jit_solution(10892957442123538138)
XLA Ops:
  0.6 29.9 %step.1 = (f32[320,960]{1,0:T(8,128)}, f32[1,960]{1,0:T(1,128)}) custom-call(f32[320,512]{1,0:T(8,128)} %bitcast.6, f32[1,512]{1,0:T(1,128)} %bitcast.8, f32[3,5]{1,0:T(4,128)} %speed_ref.1, s32[1,512]{1,0:T(1,128)} %bitcast.9, s32[384]{0:T(512)} %send_ref.1, s32[6,512]{1,0:T(8,128)} %source_ref.1, f32[64,64]{1,0:T(8,128)} %constant.2.clone.modes_ref), custom_call_target="tpu_custom_call" | custom-call | tf_op jit(solution)/shard_map/step/pallas_call | solution.py:595
  30.6 0.0 copy-start
  30.6 2.5 %copy.11 = f32[5,64,960]{2,1,0:T(8,128)} copy(f32[5,64,960]{2,1,0:T(8,128)} %bitcast.5) | data formatting | bytes 2457600
  33.1 0.0 copy-done
  33.1 0.6 %copy.12 = f32[960]{0:T(1024)} copy(f32[960]{0:T(1024)S(1)} %bitcast.7) | data formatting | bytes 7680
Async XLA Ops:
  30.6 2.5 %copy-start = (f32[1,960]{1,0:T(1,128)S(1)}, f32[1,960]{1,0:T(1,128)}, u32[]{:S(2)}) copy-start(f32[1,960]{1,0:T(1,128)} %get-tuple-element.5) | copy-start | bytes 11524

commit v2 on v1

--- a/solution.py
+++ b/solution.py
@@ -116,18 +116,22 @@
 
 def gather_sends(send_ref, trace_ref, out_ref):
     packed = jnp.broadcast_to(send_ref[...].reshape(1, 4 * SLOTS), (8, 4 * SLOTS))
-    for block in range(4):
-        shift = (4 * SLOTS - SLOTS * block) % (4 * SLOTS)
-        moved = packed if shift == 0 else pltpu.roll(packed, shift, 1)
-        index = moved[0:1, 0:LANES]
-        total = jnp.zeros((160, LANES), F32)
+    for pair in range(2):
+        moved = [
+            packed if block == 0 else pltpu.roll(packed, 4 * SLOTS - SLOTS * block, 1)
+            for block in (2 * pair, 2 * pair + 1)
+        ]
+        index = jnp.concatenate([m[0:1, 0:LANES] for m in moved], axis=1)
+        total = jnp.zeros((160, 2 * LANES), F32)
         for f in range(6):
             total = total + jnp.dot(
                 trace_ref[f],
-                one_hot(index - f * E_DEV, E_DEV, LANES),
+                one_hot(index - f * E_DEV, E_DEV, 2 * LANES),
                 preferred_element_type=F32,
             )
-        out_ref[block] = total[0:80] + total[80:160]
+        total = total[0:80] + total[80:160]
+        for half in range(2):
+            out_ref[2 * pair + half] = total[:, half * LANES : (half + 1) * LANES]
 
 
 def pair_sum(ui, um, si, sm):
@@ -332,9 +336,8 @@
     ).astype(BF16)
 
 
-def column_tables(tile, first, before, start_ref, aux_ref, coef_ref, hot_ref):
-    lane = lax.broadcasted_iota(jnp.int32, (1, LANES), 1) + first
-    place = lane.astype(F32) - 7.0 * before[0:1, :]
+def column_tables(tile, first, start_ref, aux_ref, coef_ref, hot_ref):
+    place = lax.broadcasted_iota(jnp.int32, (1, LANES), 1).astype(F32) + first
     inside = (place >= start_ref[0]) & (place < start_ref[1])
     hot = jnp.where(inside, 1.0, 0.0).astype(BF16)
     cols = pl.ds(pl.multiple_of((tile % 2) * LANES, LANES), LANES)
@@ -408,49 +411,19 @@
             put(base + 32 * h + i, combine4([coef_ref[tile, 4 * i + m] for m in range(4)], u))
 
 
-def merge(own_ref, own_jac_ref, landed_ref, out_ref, jac_ref):
-    left = lax.broadcasted_iota(jnp.int32, (8, LANES), 1) < LANES // 2
-
-    def rows_of(r, own, put):
-        low = [landed_ref[1, c, r, :] for c in range(2)]
-        far = [pltpu.roll(landed_ref[0, c, r, :], LANES // 2, 1) for c in range(2)]
-        own[0] += low[0]
-        own[1] += low[1]
-        own[5] += jnp.where(left, 0.0, far[0])
-        own[6] += jnp.where(left, far[0], far[1])
-        own[7] += far[1]
-        for c in range(8):
-            put(c, own[c])
-
-    def step(n, carry):
-        r = pl.ds(pl.multiple_of(8 * n, 8), 8)
-
-        def put(c, value):
-            if c < 7:
-                out_ref[r, c * LANES : (c + 1) * LANES] = value
-            else:
-                out_ref[r, c * LANES : E_NEW] = value[:, : E_NEW - 7 * LANES]
-
-        rows_of(r, [own_ref[c, r, :] for c in range(8)], put)
-        return carry
-
-    lax.fori_loop(0, ROWS // 8, step, 0, unroll=4)
-
-    def put_jac(c, value):
-        width = min(LANES, E_NEW - c * LANES)
-        jac_ref[0:1, c * LANES : c * LANES + width] = value[0:1, :width]
-
-    rows_of(pl.ds(ROWS, 8), [own_jac_ref[c] for c in range(8)], put_jac)
+TILES = 13
+FRAME = ROWS + 8
 
 
 def kernel(
-    x_ref, jac_ref, speed_ref, flag_ref, send_ref, source_ref, modes_ref,
-    out_ref, out_jac_ref,
+    x_hbm, jac_hbm, speed_hbm, flag_hbm, send_hbm, source_hbm, modes_hbm,
+    frame_ref, head_ref, info_ref,
+    jac_ref, speed_ref, flag_ref, send_ref, source_ref, modes_ref,
     tile_ref, trace_ref, out_buf, ghost_ref, ghost_bf, outside_ref, rate_ref, state_ref, up_ref,
-    start_ref, aux_ref, coef_ref, hot_ref, pick_ref, line_ref, own_ref, own_jac_ref,
-    blocks_ref, landed_ref, row_buf, col_buf, mine, group,
-    fetch_sems, send_sems, recv_sems, row_send, row_recv, col_send, col_recv,
-    block_send, block_recv,
+    start_ref, aux_ref, coef_ref, hot_ref, pick_ref, line_ref, tail_ref,
+    row_buf, col_buf, mine, group,
+    small_sems, fetch_sems, send_sems, recv_sems, row_send, row_recv, col_send, col_recv,
+    head_send, head_recv, tail_send, tail_recv,
 ):
     me = lax.axis_index("curve")
     devices = ROW_OF * COL_OF
@@ -458,58 +431,107 @@
     col_at = me // ROW_OF
     near = [(me + devices + o) % devices for o in (-2, -1, 1, 2)]
     row_mates = [col_at * ROW_OF + (row_at + k) % ROW_OF for k in range(1, ROW_OF)]
-    col_mates = [((col_at + k) % COL_OF) * ROW_OF + row_at for k in range(1, COL_OF)]
-    partners = near + row_mates + col_mates
     barrier = pltpu.get_barrier_semaphore()
-    for partner in partners:
+    for partner in near + row_mates:
         pl.semaphore_signal(barrier, inc=1, device_id=(partner,), device_id_type=MESH)
-    fetches = fetch_state(x_ref, tile_ref, fetch_sems)
+    for k in range(1, COL_OF):
+
+        @pl.when(col_at >= k)
+        def _(k=k):
+            pl.semaphore_signal(
+                barrier, inc=1, device_id=(me - k * ROW_OF,), device_id_type=MESH
+            )
+
+    fetches = fetch_state(x_hbm, tile_ref, fetch_sems)
+    small = []
+    for at, (src, dst) in enumerate(
+        (
+            (send_hbm, send_ref), (flag_hbm, flag_ref), (source_hbm, source_ref),
+            (jac_hbm, jac_ref), (modes_hbm, modes_ref), (speed_hbm, speed_ref),
+        )
+    ):
+        copy = pltpu.make_async_copy(src, dst, small_sems.at[at])
+        copy.start()
+        small.append(copy)
 
     def send(src, dst, send_sem, recv_sem, mate):
-        copy = pltpu.make_async_remote_copy(
+        copy = remote(src, dst, send_sem, recv_sem, mate)
+        copy.start()
+        return copy
+
+    def remote(src, dst, send_sem, recv_sem, mate):
+        return pltpu.make_async_remote_copy(
             src_ref=src, dst_ref=dst, send_sem=send_sem, recv_sem=recv_sem,
             device_id=(mate,), device_id_type=MESH,
         )
-        copy.start()
-        return copy
-
-    count = jnp.sum(flag_ref[...].astype(F32), axis=1, keepdims=True)
-    mine[...] = jnp.broadcast_to(count - 64.0, (1, LANES))
+
     for g in range(GROUPS):
         fetches[g].wait()
         build_traces(tile_ref, trace_ref, g)
+    for copy in small:
+        copy.wait()
     gather_sends(send_ref, trace_ref, out_buf)
-    pl.semaphore_wait(barrier, len(partners))
+    count = jnp.sum(flag_ref[...].astype(F32), axis=1, keepdims=True)
+    mine[...] = jnp.broadcast_to(count, (1, LANES)).astype(jnp.int32) - 64
+    pl.semaphore_wait(barrier, 4 + ROW_OF - 1 + COL_OF - 1 - col_at)
+    halo = [
+        send(out_buf.at[b], ghost_ref.at[3 - b], send_sems.at[b], recv_sems.at[3 - b], mate)
+        for b, mate in enumerate(near)
+    ]
     row_copies = [
         send(mine, row_buf.at[k], row_send.at[k], row_recv.at[k], mate)
         for k, mate in enumerate(row_mates)
     ]
-    halo = [
-        send(out_buf.at[b], ghost_ref.at[3 - b], send_sems.at[b], recv_sems.at[3 - b], mate)
-        for b, mate in enumerate(near)
-    ]
     outside_near(source_ref, trace_ref, outside_ref)
     blend_rates(tile_ref, modes_ref, jac_ref, rate_ref)
+
+    def interior_step(n, carry):
+        interior_block(n // GROUPS, n % GROUPS, tile_ref, speed_ref, rate_ref, state_ref)
+        return carry
+
+    lax.fori_loop(0, VARS * GROUPS, interior_step, 0)
+    refine_tables(flag_ref, jac_ref, start_ref, aux_ref)
+    total_new = 7.0 * jnp.broadcast_to(count, (1, LANES)) + float(E_DEV)
+
+    def table_step(tile, carry):
+        shift = (jnp.full((1, LANES), tile, jnp.int32) * LANES).astype(F32)
+        first = shift - 2.0 * LANES + jnp.where(tile < 2, total_new, 0.0)
+        jac_row = rows8(column_tables(tile, first, start_ref, aux_ref, coef_ref, hot_ref))
+
+        @pl.when(tile < 2)
+        def _():
+            tail_ref[tile, ROWS:FRAME, :] = jac_row
+
+        @pl.when(tile >= 2)
+        def _():
+            frame_ref[tile, ROWS:FRAME, :] = jac_row
+
+        return carry
+
+    lax.fori_loop(0, TILES, table_step, 0)
+
     for copy in row_copies:
         copy.wait()
     total = mine[...]
-    behind = jnp.zeros((1, LANES), F32)
+    behind = jnp.zeros((1, LANES), jnp.int32)
     for k in range(ROW_OF - 1):
         value = row_buf[k]
         total = total + value
-        behind = behind + jnp.where(row_at >= k + 1, value, 0.0)
+        behind = behind + jnp.where(row_at >= k + 1, value, 0)
     group[...] = total
     col_copies = [
-        send(group, col_buf.at[k], col_send.at[k], col_recv.at[k], mate)
-        for k, mate in enumerate(col_mates)
+        remote(
+            group, col_buf.at[k - 1], col_send.at[k - 1], col_recv.at[k - 1],
+            (me + k * ROW_OF) % devices,
+        )
+        for k in range(1, COL_OF)
     ]
-
-    def interior_step(n, carry):
-        interior_block(n // GROUPS, n % GROUPS, tile_ref, speed_ref, rate_ref, state_ref)
-        return carry
-
-    lax.fori_loop(0, VARS * GROUPS, interior_step, 0)
-    refine_tables(flag_ref, jac_ref, start_ref, aux_ref)
+    for k in range(1, COL_OF):
+
+        @pl.when(col_at + k < COL_OF)
+        def _(k=k):
+            col_copies[k - 1].start()
+
     for b in range(4):
         halo[b].wait_send()
         halo[3 - b].wait_recv()
@@ -522,62 +544,123 @@
         return carry
 
     lax.fori_loop(0, VARS * GROUPS, edge_step, 0)
-    for copy in col_copies:
-        copy.wait()
-    for k in range(COL_OF - 1):
-        behind = behind + jnp.where(col_at >= k + 1, col_buf[k], 0.0)
-
-    def table(tile, first):
-        return rows8(
-            column_tables(tile, first, behind, start_ref, aux_ref, coef_ref, hot_ref)
-        )
 
     def pick(pair):
         pick_ref[...] = jnp.dot(up_ref[...], hot_ref[pair], preferred_element_type=F32)
 
-    blocks = []
-    for at, first in enumerate((-2 * LANES, E_NEW)):
+    def fill(dst_ref, dst, tile, half):
+        def one(v, carry):
+            def put(row, value):
+                dst_ref[dst, pl.ds(row, 8, stride=4), :] = value
+
+            interpolate(v, tile, half, pick_ref, coef_ref, line_ref, put)
+            return carry
+
+        lax.fori_loop(0, VARS, one, 0)
+
+    first, last = me == 0, me == devices - 1
+    tails = [
+        remote(tail_ref.at[h], frame_ref.at[h], tail_send.at[h], tail_recv.at[h], near[2])
+        for h in range(2)
+    ]
+    heads = [
+        remote(frame_ref.at[2 + h], head_ref.at[h], head_send.at[h], head_recv.at[h], near[1])
+        for h in range(2)
+    ]
+    pick(0)
+    for half in range(2):
+        fill(tail_ref, half, half, half)
+        pl.when(jnp.logical_not(last))(tails[half].start)
+    pick(1)
+    for half in range(2):
+        fill(frame_ref, 2 + half, 2 + half, half)
+        pl.when(jnp.logical_not(first))(heads[half].start)
+
+    def own_step(pair, carry):
+        pick(pair)
         for half in range(2):
-            blocks_ref[at, half, ROWS : ROWS + 8, :] = table(2 * at + half, first + half * LANES)
-        pick(at)
-        for half in range(2):
-
-            def block_step(v, carry, at=at, half=half):
-                def put(row, value):
-                    blocks_ref[at, half, pl.ds(row, 8, stride=4), :] = value
-
-                interpolate(v, 2 * at + half, half, pick_ref, coef_ref, line_ref, put)
-                return carry
-
-            lax.fori_loop(0, VARS, block_step, 0)
-            blocks.append(
-                send(
-                    blocks_ref.at[at, half], landed_ref.at[at, half],
-                    block_send.at[2 * at + half], block_recv.at[2 * at + half], near[1 + at],
-                )
-            )
-
-    def own_step(pair, carry):
-        for half in range(2):
-            c = 2 * pair + half
-            own_jac_ref[c] = table(c + 4, c * LANES)
-        pick(pair + 2)
-        for half in range(2):
-
-            def one(v, carry, half=half):
-                def put(row, value):
-                    own_ref[2 * pair + half, pl.ds(row, 8, stride=4), :] = value
-
-                interpolate(v, 2 * pair + half + 4, half, pick_ref, coef_ref, line_ref, put)
-                return carry
-
-            lax.fori_loop(0, VARS, one, 0)
+            fill(frame_ref, 2 * pair + half, 2 * pair + half, half)
         return carry
 
-    lax.fori_loop(0, 4, own_step, 0)
-    for copy in blocks:
-        copy.wait()
-    merge(own_ref, own_jac_ref, landed_ref, out_ref, out_jac_ref)
+    lax.fori_loop(2, 6, own_step, 0)
+    pick_ref[:, 0:LANES] = jnp.dot(
+        up_ref[...], hot_ref[6, :, 0:LANES], preferred_element_type=F32
+    )
+    fill(frame_ref, TILES - 1, TILES - 1, 0)
+
+    for k in range(1, COL_OF):
+
+        @pl.when(col_at + k < COL_OF)
+        def _(k=k):
+            col_copies[k - 1].wait_send()
+
+        @pl.when(col_at >= k)
+        def _(k=k):
+            col_copies[k - 1].wait_recv()
+
+    for k in range(1, COL_OF):
+        behind = behind + jnp.where(col_at >= k, col_buf[k - 1], 0)
+    info_ref[0:1, :] = behind
+    info_ref[1:2, :] = total_new.astype(jnp.int32)
+    for half in range(2):
+
+        @pl.when(jnp.logical_not(last))
+        def _(half=half):
+            tails[half].wait_send()
+            heads[half].wait_recv()
+
+        @pl.when(jnp.logical_not(first))
+        def _(half=half):
+            heads[half].wait_send()
+            tails[half].wait_recv()
+
+
+def place_kernel(frame_ref, head_ref, info_ref, out_ref, jac_ref):
+    shift = 7 * jnp.max(info_ref[0:1, :])
+    size = jnp.max(info_ref[1:2, :])
+    begin = 2 * LANES - shift
+    tile = begin // LANES
+    turn_by = begin - tile * LANES
+    over = -(size + shift)
+    head_tile = over // LANES
+    head_turn = over - head_tile * LANES
+    lane = lax.broadcasted_iota(jnp.int32, (8, LANES), 1)
+    kept = lane < LANES - turn_by
+    head_kept = lane < LANES - head_turn
+    back = (LANES - turn_by) % LANES
+    head_back = (LANES - head_turn) % LANES
+
+    def row_tile(rows):
+        parts = [pltpu.roll(frame_ref[tile + c, rows, :], back, 1) for c in range(9)]
+        out = [jnp.where(kept, parts[c], parts[c + 1]) for c in range(8)]
+        ends = []
+        for c in range(4):
+            at = head_tile + 5 + c
+            part = pltpu.roll(head_ref[jnp.clip(at, 0, 1), rows, :], head_back, 1)
+            ends.append(jnp.where((at >= 0) & (at < 2), part, 0.0))
+        for c in range(3):
+            value = jnp.where(head_kept, ends[c], ends[c + 1])
+            out[5 + c] = out[5 + c] + value
+        return out
+
+    base = pl.program_id(0) * 64
+
+    def step(n, carry):
+        out = row_tile(pl.ds(pl.multiple_of(base + 8 * n, 8), 8))
+        rows = pl.ds(pl.multiple_of(8 * n, 8), 8)
+        for c in range(7):
+            out_ref[rows, c * LANES : (c + 1) * LANES] = out[c]
+        out_ref[rows, 7 * LANES : E_NEW] = out[7][:, : E_NEW - 7 * LANES]
+        return carry
+
+    lax.fori_loop(0, 8, step, 0, unroll=2)
+
+    @pl.when(pl.program_id(0) == 0)
+    def _():
+        out = row_tile(pl.ds(ROWS, 8))
+        for c in range(8):
+            width = min(LANES, E_NEW - c * LANES)
+            jac_ref[0:1, c * LANES : c * LANES + width] = out[c][0:1, :width]
 
 
 def vmem(count):
@@ -589,18 +672,22 @@
     jac = inverse_jacobian.reshape(1, E_DEV)
     flags = refine_flags.reshape(1, E_DEV)
     dma = pltpu.SemaphoreType.DMA
-    specs = vmem(7)
-    specs[0] = pl.BlockSpec(memory_space=pl.ANY)
-    specs[2] = pl.BlockSpec(memory_space=pltpu.SMEM)
-    out, out_jac = pl.pallas_call(
+    frame, head, info = pl.pallas_call(
         kernel,
         out_shape=(
-            jax.ShapeDtypeStruct((ROWS, E_NEW), F32),
-            jax.ShapeDtypeStruct((1, E_NEW), F32),
+            jax.ShapeDtypeStruct((TILES, FRAME, LANES), F32),
+            jax.ShapeDtypeStruct((2, FRAME, LANES), F32),
+            jax.ShapeDtypeStruct((2, LANES), jnp.int32),
         ),
-        in_specs=specs,
-        out_specs=tuple(vmem(2)),
+        in_specs=[pl.BlockSpec(memory_space=pltpu.HBM)] * 7,
+        out_specs=tuple(vmem(3)),
         scratch_shapes=[
+            pltpu.VMEM((1, E_DEV), F32),
+            pltpu.SMEM((3, VARS), F32),
+            pltpu.VMEM((1, E_DEV), jnp.int32),
+            pltpu.VMEM((4 * SLOTS,), jnp.int32),
+            pltpu.VMEM((6, E_DEV), jnp.int32),
+            pltpu.VMEM((64, 64), F32),
             pltpu.VMEM((GROUPS, ROWS, LANES), F32),
             pltpu.VMEM((6, 160, E_DEV), BF16),
             pltpu.VMEM((4, 80, LANES), F32),
@@ -612,24 +699,42 @@
             pltpu.VMEM((2 * ROWS, E_DEV), BF16),
             pltpu.VMEM((2, E_DEV, LANES), F32),
             pltpu.VMEM((16, E_DEV), BF16),
-            pltpu.VMEM((12, 40, 8, LANES), F32),
-            pltpu.VMEM((6, E_DEV, 2 * LANES), BF16),
+            pltpu.VMEM((TILES, 40, 8, LANES), F32),
+            pltpu.VMEM((7, E_DEV, 2 * LANES), BF16),
             pltpu.VMEM((2 * ROWS, 2 * LANES), F32),
             pltpu.VMEM((64, LANES), F32),
-            pltpu.VMEM((8, ROWS, LANES), F32),
-            pltpu.VMEM((8, 8, LANES), F32),
-            pltpu.VMEM((2, 2, ROWS + 8, LANES), F32),
-            pltpu.VMEM((2, 2, ROWS + 8, LANES), F32),
-            pltpu.VMEM((ROW_OF - 1, 1, LANES), F32),
-            pltpu.VMEM((COL_OF - 1, 1, LANES), F32),
-            pltpu.VMEM((1, LANES), F32),
-            pltpu.VMEM((1, LANES), F32),
-            dma((GROUPS,)), dma((4,)), dma((4,)), dma((ROW_OF - 1,)), dma((ROW_OF - 1,)),
-            dma((COL_OF - 1,)), dma((COL_OF - 1,)), dma((4,)), dma((4,)),
+            pltpu.VMEM((2, FRAME, LANES), F32),
+            pltpu.VMEM((ROW_OF - 1, 1, LANES), jnp.int32),
+            pltpu.VMEM((COL_OF - 1, 1, LANES), jnp.int32),
+            pltpu.VMEM((1, LANES), jnp.int32),
+            pltpu.VMEM((1, LANES), jnp.int32),
+            dma((6,)), dma((GROUPS,)), dma((4,)), dma((4,)), dma((ROW_OF - 1,)),
+            dma((ROW_OF - 1,)), dma((COL_OF - 1,)), dma((COL_OF - 1,)),
+            dma((2,)), dma((2,)), dma((2,)), dma((2,)),
         ],
-        compiler_params=pltpu.CompilerParams(collective_id=0, has_side_effects=True),
+        compiler_params=pltpu.CompilerParams(
+            collective_id=0, has_side_effects=True, vmem_limit_bytes=24 << 20
+        ),
         name="step",
-    )(x, jac, speeds, flags, send_index, face_source, jnp.asarray(MODES, F32))
+    )(*[
+        pltpu.with_memory_space_constraint(a, pltpu.HBM)
+        for a in (x, jac, speeds, flags, send_index, face_source, jnp.asarray(MODES, F32))
+    ])
+    out, out_jac = pl.pallas_call(
+        place_kernel,
+        grid=(VARS,),
+        out_shape=(
+            jax.ShapeDtypeStruct((ROWS, E_NEW), F32),
+            jax.ShapeDtypeStruct((1, E_NEW), F32),
+        ),
+        in_specs=vmem(3),
+        out_specs=(
+            pl.BlockSpec((64, E_NEW), lambda v: (v, 0)),
+            pl.BlockSpec((1, E_NEW), lambda v: (0, 0)),
+        ),
+        compiler_params=pltpu.CompilerParams(vmem_limit_bytes=16 << 20),
+        name="place",
+    )(frame, head, info)
     return out.reshape(VARS, 64, E_NEW), out_jac.reshape(E_NEW)
 
 

time: 33.9 us -> 29.1 us (0.86)
  the two profiles are of different devices: /device:TPU:0 before, /device:TPU:1 now
where the time goes in v2:
time: 29.1 us; the launch traced here: 29 us
  Pallas kernels  28.3 us (97%)
  between operations  0.64 us (2%)
    pallas_call x1, Pallas kernels, shards(): pl.pallas_call(kernel, out_shape=(jax.ShapeDtypeStruct((TILES, FRAME, LAN...  24.3 us
    pallas_call x1, Pallas kernels, shards(): pl.pallas_call(place_kernel, grid=(VARS,), out_shape=(jax.ShapeDtypeStruc...  4.08 us

profile of v2, /device:TPU:1, one launch (start us, length us, event | category | flops | bytes accessed | tf_op | source)
XLA Modules:
  0.0 29.0 jit_solution(15569270068035252376)
XLA Ops:
  0.6 24.3 %step.1 = (f32[13,328,128]{2,1,0:T(8,128)S(1)}, f32[2,328,128]{2,1,0:T(8,128)S(1)}, s32[2,128]{1,0:T(2,128)S(1)}) custom-call(f32[320,512]{1,0:T(8,128)} %bitcast.5, f32[1,512]{1,0:T(1,128)} %bitcast.6, f32[3,5]{1,0:T(4,128)} %speed_hbm.1, s32[1,512]{1,0:T(1,128)} %bitcast.7, s32[384]{0:T(512)} %send_hbm.1, s32[6,512]{1,0:T(8,128)} %source_hbm.1, ...), custom_call_target="tpu_custom_call" | custom-call | tf_op jit(solution)/shard_map/step/pallas_call | solution.py:675
  24.9 4.1 %place.1 = (f32[320,960]{1,0:T(8,128)}, f32[1,960]{1,0:T(1,128)}) custom-call(f32[13,328,128]{2,1,0:T(8,128)S(1)} %get-tuple-element.7.frame_ref, f32[2,328,128]{2,1,0:T(8,128)S(1)} %get-tuple-element.8.head_ref, s32[2,128]{1,0:T(2,128)S(1)} %get-tuple-element.9.info_ref), custom_call_target="tpu_custom_call" | custom-call | tf_op jit(solution)/shard_map/place/pallas_call | solution.py:723

commit v3 on v2

--- a/solution.py
+++ b/solution.py
@@ -110,8 +110,12 @@
 
 
 def one_hot(index, size, width):
-    rows = lax.broadcasted_iota(jnp.int32, (size, width), 0)
-    return jnp.where(rows == index, 1.0, 0.0).astype(BF16)
+    rows = lax.broadcasted_iota(jnp.int32, (size, width), 0).astype(jnp.int16)
+    index = jnp.broadcast_to(index, (16, width)).astype(jnp.int16)
+    index = jnp.concatenate([index] * (size // 16), axis=0)
+    return jnp.where(
+        rows == index, jnp.ones((size, width), BF16), jnp.zeros((size, width), BF16)
+    )
 
 
 def gather_sends(send_ref, trace_ref, out_ref):
@@ -185,30 +189,38 @@
         rate_ref[2:3, cols] = step
 
 
-def outside_near(source_ref, trace_ref, outside_ref):
+def outside_near(source_ref, trace_ref, far_ref, outside_ref):
     for f in range(6):
-        near_row = source_ref[f : f + 1, :] - (f ^ 1) * E_DEV
+        index = source_ref[f : f + 1, :]
         total = jnp.dot(
-            trace_ref[f ^ 1], one_hot(near_row, E_DEV, E_DEV), preferred_element_type=F32
+            trace_ref[f ^ 1],
+            one_hot(index - (f ^ 1) * E_DEV, E_DEV, E_DEV),
+            preferred_element_type=F32,
         )
         outside_ref[f] = total[0:80] + total[80:160]
-
-
-def outside_far(source_ref, ghost_ref, ghost_bf, outside_ref):
+        far = index - 6 * E_DEV
+        slot = (
+            (far >= SLOTS).astype(jnp.int32)
+            + (far >= 2 * SLOTS).astype(jnp.int32)
+            + (far >= 3 * SLOTS).astype(jnp.int32)
+        )
+        far_ref[f] = one_hot(
+            jnp.where(far >= 0, far + (LANES - SLOTS) * slot, -1), E_DEV, E_DEV
+        )
+
+
+def split_ghost(ghost_ref, ghost_bf):
     for slot in range(4):
         high, rest = split2(ghost_ref[slot])
         ghost_bf[0:80, slot * LANES : (slot + 1) * LANES] = high
         ghost_bf[80:160, slot * LANES : (slot + 1) * LANES] = rest
+
+
+def outside_far(half, far_ref, ghost_bf, outside_ref):
+    cols = pl.ds(pl.multiple_of(2 * LANES * half, 2 * LANES), 2 * LANES)
     for f in range(6):
-        far = source_ref[f : f + 1, :] - 6 * E_DEV
-        slot = (
-            (far >= SLOTS).astype(jnp.int32)
-            + (far >= 2 * SLOTS).astype(jnp.int32)
-            + (far >= 3 * SLOTS).astype(jnp.int32)
-        )
-        far_row = jnp.where(far >= 0, far + (LANES - SLOTS) * slot, -1)
-        total = jnp.dot(ghost_bf[...], one_hot(far_row, E_DEV, E_DEV), preferred_element_type=F32)
-        outside_ref[f] += total[0:80] + total[80:160]
+        total = jnp.dot(ghost_bf[...], far_ref[f, :, cols], preferred_element_type=F32)
+        outside_ref[f, :, cols] += total[0:80] + total[80:160]
 
 
 def coefs_of(d, v, speed_ref, hi, lo):
@@ -387,10 +399,11 @@
 
 
 def interpolate(v, tile, half, pick_ref, coef_ref, line_ref, put):
-    base = pl.multiple_of(64 * v, 64)
+    base = 64 * v
     cols = slice(half * LANES, half * LANES + LANES)
     tiles = [
-        pick_ref[pl.ds(base + 8 * t, 8), cols] + pick_ref[pl.ds(ROWS + base + 8 * t, 8), cols]
+        pick_ref[base + 8 * t : base + 8 * t + 8, cols]
+        + pick_ref[ROWS + base + 8 * t : ROWS + base + 8 * t + 8, cols]
         for t in range(8)
     ]
     mid = [None] * 8
@@ -402,11 +415,11 @@
         a, b = mid[2 * k], mid[2 * k + 1]
         u = [a, turn(a), b, turn(b)]
         for at in range(2):
-            line_ref[16 * k + 8 * at : 16 * k + 8 * at + 8, :] = combine4(
+            line_ref[v, 16 * k + 8 * at : 16 * k + 8 * at + 8, :] = combine4(
                 [coef_ref[tile, 32 + 4 * at + m] for m in range(4)], u
             )
     for h in range(2):
-        u = [line_ref[pl.ds(32 * h + i, 8, stride=4), :] for i in range(4)]
+        u = [line_ref[v, pl.ds(32 * h + i, 8, stride=4), :] for i in range(4)]
         for i in range(4):
             put(base + 32 * h + i, combine4([coef_ref[tile, 4 * i + m] for m in range(4)], u))
 
@@ -420,7 +433,7 @@
     frame_ref, head_ref, info_ref,
     jac_ref, speed_ref, flag_ref, send_ref, source_ref, modes_ref,
     tile_ref, trace_ref, out_buf, ghost_ref, ghost_bf, outside_ref, rate_ref, state_ref, up_ref,
-    start_ref, aux_ref, coef_ref, hot_ref, pick_ref, line_ref, tail_ref,
+    start_ref, aux_ref, coef_ref, hot_ref, pick_a, pick_b, line_ref, far_ref,
     row_buf, col_buf, mine, group,
     small_sems, fetch_sems, send_sems, recv_sems, row_send, row_recv, col_send, col_recv,
     head_send, head_recv, tail_send, tail_recv,
@@ -482,7 +495,7 @@
         send(mine, row_buf.at[k], row_send.at[k], row_recv.at[k], mate)
         for k, mate in enumerate(row_mates)
     ]
-    outside_near(source_ref, trace_ref, outside_ref)
+    outside_near(source_ref, trace_ref, far_ref, outside_ref)
     blend_rates(tile_ref, modes_ref, jac_ref, rate_ref)
 
     def interior_step(n, carry):
@@ -497,15 +510,7 @@
         shift = (jnp.full((1, LANES), tile, jnp.int32) * LANES).astype(F32)
         first = shift - 2.0 * LANES + jnp.where(tile < 2, total_new, 0.0)
         jac_row = rows8(column_tables(tile, first, start_ref, aux_ref, coef_ref, hot_ref))
-
-        @pl.when(tile < 2)
-        def _():
-            tail_ref[tile, ROWS:FRAME, :] = jac_row
-
-        @pl.when(tile >= 2)
-        def _():
-            frame_ref[tile, ROWS:FRAME, :] = jac_row
-
+        frame_ref[jnp.where(tile < 2, TILES + tile, tile), ROWS:FRAME, :] = jac_row
         return carry
 
     lax.fori_loop(0, TILES, table_step, 0)
@@ -535,58 +540,62 @@
     for b in range(4):
         halo[b].wait_send()
         halo[3 - b].wait_recv()
-    outside_far(source_ref, ghost_ref, ghost_bf, outside_ref)
-
-    def edge_step(n, carry):
-        edge_block(
-            n // GROUPS, n % GROUPS, tile_ref, speed_ref, rate_ref, outside_ref, state_ref, up_ref
-        )
-        return carry
-
-    lax.fori_loop(0, VARS * GROUPS, edge_step, 0)
-
-    def pick(pair):
-        pick_ref[...] = jnp.dot(up_ref[...], hot_ref[pair], preferred_element_type=F32)
-
-    def fill(dst_ref, dst, tile, half):
-        def one(v, carry):
-            def put(row, value):
-                dst_ref[dst, pl.ds(row, 8, stride=4), :] = value
-
-            interpolate(v, tile, half, pick_ref, coef_ref, line_ref, put)
-            return carry
-
-        lax.fori_loop(0, VARS, one, 0)
-
+    split_ghost(ghost_ref, ghost_bf)
     first, last = me == 0, me == devices - 1
     tails = [
-        remote(tail_ref.at[h], frame_ref.at[h], tail_send.at[h], tail_recv.at[h], near[2])
+        remote(
+            frame_ref.at[TILES + h], frame_ref.at[h], tail_send.at[h], tail_recv.at[h], near[2]
+        )
         for h in range(2)
     ]
     heads = [
         remote(frame_ref.at[2 + h], head_ref.at[h], head_send.at[h], head_recv.at[h], near[1])
         for h in range(2)
     ]
-    pick(0)
-    for half in range(2):
-        fill(tail_ref, half, half, half)
-        pl.when(jnp.logical_not(last))(tails[half].start)
-    pick(1)
-    for half in range(2):
-        fill(frame_ref, 2 + half, 2 + half, half)
-        pl.when(jnp.logical_not(first))(heads[half].start)
-
-    def own_step(pair, carry):
-        pick(pair)
+
+    def fill(dst, tile, half, pick_ref):
+        for v in range(VARS):
+
+            def put(row, value):
+                frame_ref[dst, pl.ds(row, 8, stride=4), :] = value
+
+            interpolate(v, tile, half, pick_ref, coef_ref, line_ref, put)
+
+    for order in range(2):
+        part = me % 2 if order == 0 else 1 - me % 2
+        outside_far(part, far_ref, ghost_bf, outside_ref)
+
+        def edge_step(n, carry, part=part):
+            edge_block(
+                n // 2, 2 * part + n % 2, tile_ref, speed_ref, rate_ref, outside_ref, state_ref,
+                up_ref,
+            )
+            return carry
+
+        lax.fori_loop(0, 2 * VARS, edge_step, 0)
+        within = pl.ds(pl.multiple_of(2 * LANES * part, 2 * LANES), 2 * LANES)
+        pick_a[...] = jnp.dot(
+            up_ref[:, within], hot_ref[1 - part, within, :], preferred_element_type=F32
+        )
         for half in range(2):
-            fill(frame_ref, 2 * pair + half, 2 * pair + half, half)
-        return carry
-
-    lax.fori_loop(2, 6, own_step, 0)
-    pick_ref[:, 0:LANES] = jnp.dot(
-        up_ref[...], hot_ref[6, :, 0:LANES], preferred_element_type=F32
-    )
-    fill(frame_ref, TILES - 1, TILES - 1, 0)
+            fill(
+                jnp.where(part == 1, TILES, 2) + half, 2 * (1 - part) + half, half, pick_a
+            )
+            pl.when((part == 1) & jnp.logical_not(last))(tails[half].start)
+            pl.when((part == 0) & jnp.logical_not(first))(heads[half].start)
+
+    picks = [pick_a, pick_b]
+    pick_a[...] = jnp.dot(up_ref[...], hot_ref[2], preferred_element_type=F32)
+    for pair in range(2, 7):
+        now, later = picks[pair % 2], picks[(pair + 1) % 2]
+        if pair < 5:
+            later[...] = jnp.dot(up_ref[...], hot_ref[pair + 1], preferred_element_type=F32)
+        if pair == 5:
+            later[:, 0:LANES] = jnp.dot(
+                up_ref[...], hot_ref[6, :, 0:LANES], preferred_element_type=F32
+            )
+        for half in range(2 if pair < 6 else 1):
+            fill(2 * pair + half, 2 * pair + half, half, now)
 
     for k in range(1, COL_OF):
 
@@ -615,7 +624,10 @@
             tails[half].wait_recv()
 
 
-def place_kernel(frame_ref, head_ref, info_ref, out_ref, jac_ref):
+CHUNK = 64
+
+
+def place_kernel(frame_ref, head_ref, info_ref, out_hbm, jac_hbm, out_ref, jac_ref, sems):
     shift = 7 * jnp.max(info_ref[0:1, :])
     size = jnp.max(info_ref[1:2, :])
     begin = 2 * LANES - shift
@@ -639,28 +651,28 @@
             part = pltpu.roll(head_ref[jnp.clip(at, 0, 1), rows, :], head_back, 1)
             ends.append(jnp.where((at >= 0) & (at < 2), part, 0.0))
         for c in range(3):
-            value = jnp.where(head_kept, ends[c], ends[c + 1])
-            out[5 + c] = out[5 + c] + value
+            out[5 + c] = out[5 + c] + jnp.where(head_kept, ends[c], ends[c + 1])
         return out
 
-    base = pl.program_id(0) * 64
-
-    def step(n, carry):
-        out = row_tile(pl.ds(pl.multiple_of(base + 8 * n, 8), 8))
-        rows = pl.ds(pl.multiple_of(8 * n, 8), 8)
-        for c in range(7):
-            out_ref[rows, c * LANES : (c + 1) * LANES] = out[c]
-        out_ref[rows, 7 * LANES : E_NEW] = out[7][:, : E_NEW - 7 * LANES]
-        return carry
-
-    lax.fori_loop(0, 8, step, 0, unroll=2)
-
-    @pl.when(pl.program_id(0) == 0)
-    def _():
-        out = row_tile(pl.ds(ROWS, 8))
-        for c in range(8):
-            width = min(LANES, E_NEW - c * LANES)
-            jac_ref[0:1, c * LANES : c * LANES + width] = out[c][0:1, :width]
+    out = row_tile(pl.ds(ROWS, 8))
+    for c in range(8):
+        width = min(LANES, E_NEW - c * LANES)
+        jac_ref[0:1, c * LANES : c * LANES + width] = out[c][0:1, :width]
+    copies = [pltpu.make_async_copy(jac_ref, jac_hbm, sems.at[ROWS // CHUNK])]
+    copies[0].start()
+    for chunk in range(ROWS // CHUNK):
+        for n in range(CHUNK // 8):
+            row = chunk * CHUNK + 8 * n
+            out = row_tile(pl.ds(row, 8))
+            for c in range(7):
+                out_ref[row : row + 8, c * LANES : (c + 1) * LANES] = out[c]
+            out_ref[row : row + 8, 7 * LANES : E_NEW] = out[7][:, : E_NEW - 7 * LANES]
+        rows = pl.ds(chunk * CHUNK, CHUNK)
+        copy = pltpu.make_async_copy(out_ref.at[rows], out_hbm.at[rows], sems.at[chunk])
+        copy.start()
+        copies.append(copy)
+    for copy in copies:
+        copy.wait()
 
 
 def vmem(count):
@@ -675,7 +687,7 @@
     frame, head, info = pl.pallas_call(
         kernel,
         out_shape=(
-            jax.ShapeDtypeStruct((TILES, FRAME, LANES), F32),
+            jax.ShapeDtypeStruct((TILES + 2, FRAME, LANES), F32),
             jax.ShapeDtypeStruct((2, FRAME, LANES), F32),
             jax.ShapeDtypeStruct((2, LANES), jnp.int32),
         ),
@@ -702,8 +714,9 @@
             pltpu.VMEM((TILES, 40, 8, LANES), F32),
             pltpu.VMEM((7, E_DEV, 2 * LANES), BF16),
             pltpu.VMEM((2 * ROWS, 2 * LANES), F32),
-            pltpu.VMEM((64, LANES), F32),
-            pltpu.VMEM((2, FRAME, LANES), F32),
+            pltpu.VMEM((2 * ROWS, 2 * LANES), F32),
+            pltpu.VMEM((VARS, 64, LANES), F32),
+            pltpu.VMEM((6, E_DEV, E_DEV), BF16),
             pltpu.VMEM((ROW_OF - 1, 1, LANES), jnp.int32),
             pltpu.VMEM((COL_OF - 1, 1, LANES), jnp.int32),
             pltpu.VMEM((1, LANES), jnp.int32),
@@ -713,7 +726,7 @@
             dma((2,)), dma((2,)), dma((2,)), dma((2,)),
         ],
         compiler_params=pltpu.CompilerParams(
-            collective_id=0, has_side_effects=True, vmem_limit_bytes=24 << 20
+            collective_id=0, has_side_effects=True, vmem_limit_bytes=28 << 20
         ),
         name="step",
     )(*[
@@ -722,16 +735,17 @@
     ])
     out, out_jac = pl.pallas_call(
         place_kernel,
-        grid=(VARS,),
         out_shape=(
             jax.ShapeDtypeStruct((ROWS, E_NEW), F32),
             jax.ShapeDtypeStruct((1, E_NEW), F32),
         ),
         in_specs=vmem(3),
         out_specs=(
-            pl.BlockSpec((64, E_NEW), lambda v: (v, 0)),
-            pl.BlockSpec((1, E_NEW), lambda v: (0, 0)),
+            pl.BlockSpec(memory_space=pltpu.HBM), pl.BlockSpec(memory_space=pltpu.HBM)
         ),
+        scratch_shapes=[
+            pltpu.VMEM((ROWS, E_NEW), F32), pltpu.VMEM((1, E_NEW), F32), dma((ROWS // CHUNK + 1,))
+        ],
         compiler_params=pltpu.CompilerParams(vmem_limit_bytes=16 << 20),
         name="place",
     )(frame, head, info)

time: 29.1 us -> 24.7 us (0.85)
  Pallas kernels: 28.3 us -> 23.9 us
    pallas_call x2, Pallas kernels: 28.3 us -> 23.9 us  [the longest x1 22.3 us: shards(): pl.pallas_call(kernel, out_shape=(jax.ShapeDtypeStruct((TILES + 2, FRAME,...]
where the time goes in v3:
time: 24.7 us; the launch traced here: 24.5 us
  Pallas kernels  23.9 us (97%)
  between operations  0.64 us (3%)
    pallas_call x1, Pallas kernels, shards(): pl.pallas_call(kernel, out_shape=(jax.ShapeDtypeStruct((TILES + 2, FRAME,...  22.3 us
    pallas_call x1, Pallas kernels, shards(): pl.pallas_call(place_kernel, out_shape=(jax.ShapeDtypeStruct((ROWS, E_NEW...  1.6 us

profile of v3, /device:TPU:1, one launch (start us, length us, event | category | flops | bytes accessed | tf_op | source)
XLA Modules:
  0.0 24.5 jit_solution(4515324051676357045)
XLA Ops:
  0.6 22.3 %step.1 = (f32[15,328,128]{2,1,0:T(8,128)S(1)}, f32[2,328,128]{2,1,0:T(8,128)S(1)}, s32[2,128]{1,0:T(2,128)S(1)}) custom-call(f32[320,512]{1,0:T(8,128)} %bitcast.5, f32[1,512]{1,0:T(1,128)} %bitcast.6, f32[3,5]{1,0:T(4,128)} %speed_hbm.1, s32[1,512]{1,0:T(1,128)} %bitcast.7, s32[384]{0:T(512)} %send_hbm.1, s32[6,512]{1,0:T(8,128)} %source_hbm.1, ...), custom_call_target="tpu_custom_call" | custom-call | tf_op jit(solution)/shard_map/step/pallas_call | solution.py:687
  22.9 1.6 %place.1 = (f32[320,960]{1,0:T(8,128)}, f32[1,960]{1,0:T(1,128)}) custom-call(f32[15,328,128]{2,1,0:T(8,128)S(1)} %get-tuple-element.7.frame_ref, f32[2,328,128]{2,1,0:T(8,128)S(1)} %get-tuple-element.8.head_ref, s32[2,128]{1,0:T(2,128)S(1)} %get-tuple-element.9.info_ref), custom_call_target="tpu_custom_call" | custom-call | tf_op jit(solution)/shard_map/place/pallas_call | solution.py:736

commit v4 on v3

--- a/solution.py
+++ b/solution.py
@@ -18,7 +18,7 @@
 LANES = 128
 GROUPS = E_DEV // LANES
 ROW_OF = 8
-COL_OF = 16
+SIDE = 4
 F32 = jnp.float32
 BF16 = jnp.bfloat16
 MESH = pl.DeviceIdType.MESH
@@ -434,28 +434,34 @@
     jac_ref, speed_ref, flag_ref, send_ref, source_ref, modes_ref,
     tile_ref, trace_ref, out_buf, ghost_ref, ghost_bf, outside_ref, rate_ref, state_ref, up_ref,
     start_ref, aux_ref, coef_ref, hot_ref, pick_a, pick_b, line_ref, far_ref,
-    row_buf, col_buf, mine, group,
-    small_sems, fetch_sems, send_sems, recv_sems, row_send, row_recv, col_send, col_recv,
+    row_buf, z_buf, y_buf, mine, row_sum, plane_sum,
+    small_sems, fetch_sems, send_sems, recv_sems, row_send, row_recv, z_send, z_recv,
+    y_send, y_recv,
     head_send, head_recv, tail_send, tail_recv,
 ):
     me = lax.axis_index("curve")
-    devices = ROW_OF * COL_OF
+    devices = ROW_OF * SIDE * SIDE
     row_at = me % ROW_OF
-    col_at = me // ROW_OF
+    z_at = me // ROW_OF % SIDE
+    y_at = me // (ROW_OF * SIDE)
     near = [(me + devices + o) % devices for o in (-2, -1, 1, 2)]
-    row_mates = [col_at * ROW_OF + (row_at + k) % ROW_OF for k in range(1, ROW_OF)]
+    row_mates = [me - row_at + (row_at + k) % ROW_OF for k in range(1, ROW_OF)]
+    z_mates = [me + ROW_OF * ((z_at + k) % SIDE - z_at) for k in range(1, SIDE)]
+    early = me < 2
     barrier = pltpu.get_barrier_semaphore()
-    for partner in near + row_mates:
+    for partner in near:
         pl.semaphore_signal(barrier, inc=1, device_id=(partner,), device_id_type=MESH)
-    for k in range(1, COL_OF):
-
-        @pl.when(col_at >= k)
+    fetches = fetch_state(x_hbm, tile_ref, fetch_sems)
+    for partner in row_mates + z_mates:
+        pl.semaphore_signal(barrier, inc=1, device_id=(partner,), device_id_type=MESH)
+    for k in range(1, SIDE):
+
+        @pl.when(y_at >= k)
         def _(k=k):
             pl.semaphore_signal(
-                barrier, inc=1, device_id=(me - k * ROW_OF,), device_id_type=MESH
+                barrier, inc=1, device_id=(me - k * ROW_OF * SIDE,), device_id_type=MESH
             )
 
-    fetches = fetch_state(x_hbm, tile_ref, fetch_sems)
     small = []
     for at, (src, dst) in enumerate(
         (
@@ -486,7 +492,30 @@
     gather_sends(send_ref, trace_ref, out_buf)
     count = jnp.sum(flag_ref[...].astype(F32), axis=1, keepdims=True)
     mine[...] = jnp.broadcast_to(count, (1, LANES)).astype(jnp.int32) - 64
-    pl.semaphore_wait(barrier, 4 + ROW_OF - 1 + COL_OF - 1 - col_at)
+    total_new = 7.0 * jnp.broadcast_to(count, (1, LANES)) + float(E_DEV)
+
+    def local_work():
+        outside_near(source_ref, trace_ref, far_ref, outside_ref)
+        blend_rates(tile_ref, modes_ref, jac_ref, rate_ref)
+
+        def interior_step(n, carry):
+            interior_block(n // GROUPS, n % GROUPS, tile_ref, speed_ref, rate_ref, state_ref)
+            return carry
+
+        lax.fori_loop(0, VARS * GROUPS, interior_step, 0)
+        refine_tables(flag_ref, jac_ref, start_ref, aux_ref)
+
+        def table_step(tile, carry):
+            shift = (jnp.full((1, LANES), tile, jnp.int32) * LANES).astype(F32)
+            first = shift - 2.0 * LANES + jnp.where(tile < 2, total_new, 0.0)
+            jac_row = rows8(column_tables(tile, first, start_ref, aux_ref, coef_ref, hot_ref))
+            frame_ref[jnp.where(tile < 2, TILES + tile, tile), ROWS:FRAME, :] = jac_row
+            return carry
+
+        lax.fori_loop(0, TILES, table_step, 0)
+
+    pl.when(early)(local_work)
+    pl.semaphore_wait(barrier, 4 + ROW_OF - 1 + SIDE - 1 + SIDE - 1 - y_at)
     halo = [
         send(out_buf.at[b], ghost_ref.at[3 - b], send_sems.at[b], recv_sems.at[3 - b], mate)
         for b, mate in enumerate(near)
@@ -495,48 +524,26 @@
         send(mine, row_buf.at[k], row_send.at[k], row_recv.at[k], mate)
         for k, mate in enumerate(row_mates)
     ]
-    outside_near(source_ref, trace_ref, far_ref, outside_ref)
-    blend_rates(tile_ref, modes_ref, jac_ref, rate_ref)
-
-    def interior_step(n, carry):
-        interior_block(n // GROUPS, n % GROUPS, tile_ref, speed_ref, rate_ref, state_ref)
-        return carry
-
-    lax.fori_loop(0, VARS * GROUPS, interior_step, 0)
-    refine_tables(flag_ref, jac_ref, start_ref, aux_ref)
-    total_new = 7.0 * jnp.broadcast_to(count, (1, LANES)) + float(E_DEV)
-
-    def table_step(tile, carry):
-        shift = (jnp.full((1, LANES), tile, jnp.int32) * LANES).astype(F32)
-        first = shift - 2.0 * LANES + jnp.where(tile < 2, total_new, 0.0)
-        jac_row = rows8(column_tables(tile, first, start_ref, aux_ref, coef_ref, hot_ref))
-        frame_ref[jnp.where(tile < 2, TILES + tile, tile), ROWS:FRAME, :] = jac_row
-        return carry
-
-    lax.fori_loop(0, TILES, table_step, 0)
-
-    for copy in row_copies:
-        copy.wait()
-    total = mine[...]
-    behind = jnp.zeros((1, LANES), jnp.int32)
-    for k in range(ROW_OF - 1):
-        value = row_buf[k]
-        total = total + value
-        behind = behind + jnp.where(row_at >= k + 1, value, 0)
-    group[...] = total
-    col_copies = [
-        remote(
-            group, col_buf.at[k - 1], col_send.at[k - 1], col_recv.at[k - 1],
-            (me + k * ROW_OF) % devices,
-        )
-        for k in range(1, COL_OF)
+    pl.when(jnp.logical_not(early))(local_work)
+
+    def gathered(copies, own_ref, buf_ref, at, behind):
+        for copy in copies:
+            copy.wait()
+        total = own_ref[...]
+        for k in range(len(copies)):
+            value = buf_ref[k]
+            total = total + value
+            behind = behind + jnp.where(at >= k + 1, value, 0)
+        return total, behind
+
+    total, behind = gathered(
+        row_copies, mine, row_buf, row_at, jnp.zeros((1, LANES), jnp.int32)
+    )
+    row_sum[...] = total
+    z_copies = [
+        send(row_sum, z_buf.at[k], z_send.at[k], z_recv.at[k], mate)
+        for k, mate in enumerate(z_mates)
     ]
-    for k in range(1, COL_OF):
-
-        @pl.when(col_at + k < COL_OF)
-        def _(k=k):
-            col_copies[k - 1].start()
-
     for b in range(4):
         halo[b].wait_send()
         halo[3 - b].wait_recv()
@@ -583,6 +590,18 @@
             )
             pl.when((part == 1) & jnp.logical_not(last))(tails[half].start)
             pl.when((part == 0) & jnp.logical_not(first))(heads[half].start)
+
+    total, behind = gathered(z_copies, row_sum, z_buf, z_at, behind)
+    plane_sum[...] = total
+    y_copies = [
+        remote(
+            plane_sum, y_buf.at[k - 1], y_send.at[k - 1], y_recv.at[k - 1],
+            (me + k * ROW_OF * SIDE) % devices,
+        )
+        for k in range(1, SIDE)
+    ]
+    for k in range(1, SIDE):
+        pl.when(y_at + k < SIDE)(y_copies[k - 1].start)
 
     picks = [pick_a, pick_b]
     pick_a[...] = jnp.dot(up_ref[...], hot_ref[2], preferred_element_type=F32)
@@ -597,18 +616,10 @@
         for half in range(2 if pair < 6 else 1):
             fill(2 * pair + half, 2 * pair + half, half, now)
 
-    for k in range(1, COL_OF):
-
-        @pl.when(col_at + k < COL_OF)
-        def _(k=k):
-            col_copies[k - 1].wait_send()
-
-        @pl.when(col_at >= k)
-        def _(k=k):
-            col_copies[k - 1].wait_recv()
-
-    for k in range(1, COL_OF):
-        behind = behind + jnp.where(col_at >= k, col_buf[k - 1], 0)
+    for k in range(1, SIDE):
+        pl.when(y_at + k < SIDE)(y_copies[k - 1].wait_send)
+        pl.when(y_at >= k)(y_copies[k - 1].wait_recv)
+        behind = behind + jnp.where(y_at >= k, y_buf[k - 1], 0)
     info_ref[0:1, :] = behind
     info_ref[1:2, :] = total_new.astype(jnp.int32)
     for half in range(2):
@@ -718,11 +729,14 @@
             pltpu.VMEM((VARS, 64, LANES), F32),
             pltpu.VMEM((6, E_DEV, E_DEV), BF16),
             pltpu.VMEM((ROW_OF - 1, 1, LANES), jnp.int32),
-            pltpu.VMEM((COL_OF - 1, 1, LANES), jnp.int32),
+            pltpu.VMEM((SIDE - 1, 1, LANES), jnp.int32),
+            pltpu.VMEM((SIDE - 1, 1, LANES), jnp.int32),
+            pltpu.VMEM((1, LANES), jnp.int32),
             pltpu.VMEM((1, LANES), jnp.int32),
             pltpu.VMEM((1, LANES), jnp.int32),
             dma((6,)), dma((GROUPS,)), dma((4,)), dma((4,)), dma((ROW_OF - 1,)),
-            dma((ROW_OF - 1,)), dma((COL_OF - 1,)), dma((COL_OF - 1,)),
+            dma((ROW_OF - 1,)), dma((SIDE - 1,)), dma((SIDE - 1,)), dma((SIDE - 1,)),
+            dma((SIDE - 1,)),
             dma((2,)), dma((2,)), dma((2,)), dma((2,)),
         ],
         compiler_params=pltpu.CompilerParams(

time: 24.7 us -> 23.6 us (0.955)
  the two profiles are of different devices: /device:TPU:1 before, /device:TPU:24 now
where the time goes in v4:
time: 23.6 us; the launch traced here: 23.5 us
  Pallas kernels  22.9 us (97%)
  between operations  0.64 us (3%)
    pallas_call x1, Pallas kernels, shards(): pl.pallas_call(kernel, out_shape=(jax.ShapeDtypeStruct((TILES + 2, FRAME,...  21.3 us
    pallas_call x1, Pallas kernels, shards(): pl.pallas_call(place_kernel, out_shape=(jax.ShapeDtypeStruct((ROWS, E_NEW...  1.6 us

profile of v4, /device:TPU:24, one launch (start us, length us, event | category | flops | bytes accessed | tf_op | source)
XLA Modules:
  0.0 23.5 jit_solution(8968926113454748098)
XLA Ops:
  0.6 21.3 %step.1 = (f32[15,328,128]{2,1,0:T(8,128)S(1)}, f32[2,328,128]{2,1,0:T(8,128)S(1)}, s32[2,128]{1,0:T(2,128)S(1)}) custom-call(f32[320,512]{1,0:T(8,128)} %bitcast.5, f32[1,512]{1,0:T(1,128)} %bitcast.6, f32[3,5]{1,0:T(4,128)} %speed_hbm.1, s32[1,512]{1,0:T(1,128)} %bitcast.7, s32[384]{0:T(512)} %send_hbm.1, s32[6,512]{1,0:T(8,128)} %source_hbm.1, ...), custom_call_target="tpu_custom_call" | custom-call | tf_op jit(solution)/shard_map/step/pallas_call | solution.py:698
  21.9 1.6 %place.1 = (f32[320,960]{1,0:T(8,128)}, f32[1,960]{1,0:T(1,128)}) custom-call(f32[15,328,128]{2,1,0:T(8,128)S(1)} %get-tuple-element.7.frame_ref, f32[2,328,128]{2,1,0:T(8,128)S(1)} %get-tuple-element.8.head_ref, s32[2,128]{1,0:T(2,128)S(1)} %get-tuple-element.9.info_ref), custom_call_target="tpu_custom_call" | custom-call | tf_op jit(solution)/shard_map/place/pallas_call | solution.py:750

commit v5 on v4

--- a/solution.py
+++ b/solution.py
@@ -434,10 +434,10 @@
     jac_ref, speed_ref, flag_ref, send_ref, source_ref, modes_ref,
     tile_ref, trace_ref, out_buf, ghost_ref, ghost_bf, outside_ref, rate_ref, state_ref, up_ref,
     start_ref, aux_ref, coef_ref, hot_ref, pick_a, pick_b, line_ref, far_ref,
-    row_buf, z_buf, y_buf, mine, row_sum, plane_sum,
+    row_buf, z_buf, y_buf, mine, row_sum, plane_sum, behind_ref,
     small_sems, fetch_sems, send_sems, recv_sems, row_send, row_recv, z_send, z_recv,
     y_send, y_recv,
-    head_send, head_recv, tail_send, tail_recv,
+    head_send, head_recv, tail_send, tail_recv, reply,
 ):
     me = lax.axis_index("curve")
     devices = ROW_OF * SIDE * SIDE
@@ -447,10 +447,15 @@
     near = [(me + devices + o) % devices for o in (-2, -1, 1, 2)]
     row_mates = [me - row_at + (row_at + k) % ROW_OF for k in range(1, ROW_OF)]
     z_mates = [me + ROW_OF * ((z_at + k) % SIDE - z_at) for k in range(1, SIDE)]
-    early = me < 2
+    early = me % (ROW_OF * SIDE) < 2
+    awaited = me >= devices - 4
     barrier = pltpu.get_barrier_semaphore()
-    for partner in near:
-        pl.semaphore_signal(barrier, inc=1, device_id=(partner,), device_id_type=MESH)
+    for b, partner in enumerate(near):
+
+        @pl.when(me + (-2, -1, 1, 2)[b] < devices)
+        def _(partner=partner):
+            pl.semaphore_signal(barrier, inc=1, device_id=(partner,), device_id_type=MESH)
+
     fetches = fetch_state(x_hbm, tile_ref, fetch_sems)
     for partner in row_mates + z_mates:
         pl.semaphore_signal(barrier, inc=1, device_id=(partner,), device_id_type=MESH)
@@ -487,78 +492,116 @@
     for g in range(GROUPS):
         fetches[g].wait()
         build_traces(tile_ref, trace_ref, g)
-    for copy in small:
+    small[0].wait()
+    gather_sends(send_ref, trace_ref, out_buf)
+    for copy in small[1:]:
         copy.wait()
-    gather_sends(send_ref, trace_ref, out_buf)
     count = jnp.sum(flag_ref[...].astype(F32), axis=1, keepdims=True)
     mine[...] = jnp.broadcast_to(count, (1, LANES)).astype(jnp.int32) - 64
     total_new = 7.0 * jnp.broadcast_to(count, (1, LANES)) + float(E_DEV)
 
-    def local_work():
+    def near_work():
         outside_near(source_ref, trace_ref, far_ref, outside_ref)
         blend_rates(tile_ref, modes_ref, jac_ref, rate_ref)
 
+    def table_step(tile, carry):
+        shift = (jnp.full((1, LANES), tile, jnp.int32) * LANES).astype(F32)
+        first = shift - 2.0 * LANES + jnp.where(tile < 2, total_new, 0.0)
+        jac_row = rows8(column_tables(tile, first, start_ref, aux_ref, coef_ref, hot_ref))
+        frame_ref[jnp.where(tile < 2, TILES + tile, tile), ROWS:FRAME, :] = jac_row
+        return carry
+
+    def inner_work():
         def interior_step(n, carry):
             interior_block(n // GROUPS, n % GROUPS, tile_ref, speed_ref, rate_ref, state_ref)
             return carry
 
         lax.fori_loop(0, VARS * GROUPS, interior_step, 0)
         refine_tables(flag_ref, jac_ref, start_ref, aux_ref)
-
-        def table_step(tile, carry):
-            shift = (jnp.full((1, LANES), tile, jnp.int32) * LANES).astype(F32)
-            first = shift - 2.0 * LANES + jnp.where(tile < 2, total_new, 0.0)
-            jac_row = rows8(column_tables(tile, first, start_ref, aux_ref, coef_ref, hot_ref))
-            frame_ref[jnp.where(tile < 2, TILES + tile, tile), ROWS:FRAME, :] = jac_row
-            return carry
-
-        lax.fori_loop(0, TILES, table_step, 0)
-
-    pl.when(early)(local_work)
-    pl.semaphore_wait(barrier, 4 + ROW_OF - 1 + SIDE - 1 + SIDE - 1 - y_at)
-    halo = [
-        send(out_buf.at[b], ghost_ref.at[3 - b], send_sems.at[b], recv_sems.at[3 - b], mate)
-        for b, mate in enumerate(near)
-    ]
+        lax.fori_loop(0, 4, table_step, 0)
+
+    def own_tables():
+        lax.fori_loop(4, TILES, table_step, 0)
+
+    pl.when(jnp.logical_not(awaited))(near_work)
+    pl.when(early)(inner_work)
+    pl.semaphore_wait(
+        barrier, 4 - jnp.maximum(2 - me, 0) + ROW_OF - 1 + SIDE - 1 + SIDE - 1 - y_at
+    )
+    for b in (2, 3):
+
+        @pl.when(me + b - 1 >= devices)
+        def _(b=b):
+            pl.semaphore_signal(reply, inc=1, device_id=(near[b],), device_id_type=MESH)
+
+    halo = {
+        b: remote(
+            out_buf.at[b], ghost_ref.at[3 - b], send_sems.at[b], recv_sems.at[3 - b], near[b]
+        )
+        for b in (1, 3, 0, 2)
+    }
+    for b in (1, 3, 0, 2):
+        pl.when(me >= 2 - b)(halo[b].start)
     row_copies = [
         send(mine, row_buf.at[k], row_send.at[k], row_recv.at[k], mate)
         for k, mate in enumerate(row_mates)
     ]
-    pl.when(jnp.logical_not(early))(local_work)
-
-    def gathered(copies, own_ref, buf_ref, at, behind):
+    pl.when(awaited)(near_work)
+    pl.when(jnp.logical_not(early))(inner_work)
+    pl.when(early)(own_tables)
+
+    @pl.when(me < 2)
+    def _():
+        pl.semaphore_wait(reply, 2 - me)
+        for b in range(2):
+            pl.when(me < 2 - b)(halo[b].start)
+
+    def gathered(copies, own_ref, buf_ref, at, sum_ref):
         for copy in copies:
             copy.wait()
         total = own_ref[...]
+        behind = behind_ref[...]
         for k in range(len(copies)):
             value = buf_ref[k]
             total = total + value
             behind = behind + jnp.where(at >= k + 1, value, 0)
-        return total, behind
-
-    total, behind = gathered(
-        row_copies, mine, row_buf, row_at, jnp.zeros((1, LANES), jnp.int32)
-    )
-    row_sum[...] = total
+        sum_ref[...] = total
+        behind_ref[...] = behind
+
+    behind_ref[...] = jnp.zeros((1, LANES), jnp.int32)
     z_copies = [
-        send(row_sum, z_buf.at[k], z_send.at[k], z_recv.at[k], mate)
+        remote(row_sum, z_buf.at[k], z_send.at[k], z_recv.at[k], mate)
         for k, mate in enumerate(z_mates)
     ]
+    y_copies = [
+        remote(
+            plane_sum, y_buf.at[k - 1], y_send.at[k - 1], y_recv.at[k - 1],
+            (me + k * ROW_OF * SIDE) % devices,
+        )
+        for k in range(1, SIDE)
+    ]
+
+    def row_stage():
+        gathered(row_copies, mine, row_buf, row_at, row_sum)
+        for copy in z_copies:
+            copy.start()
+
+    row_stage()
     for b in range(4):
         halo[b].wait_send()
         halo[3 - b].wait_recv()
     split_ghost(ghost_ref, ghost_bf)
     first, last = me == 0, me == devices - 1
-    tails = [
-        remote(
+
+    def tail(h):
+        return remote(
             frame_ref.at[TILES + h], frame_ref.at[h], tail_send.at[h], tail_recv.at[h], near[2]
         )
-        for h in range(2)
-    ]
-    heads = [
-        remote(frame_ref.at[2 + h], head_ref.at[h], head_send.at[h], head_recv.at[h], near[1])
-        for h in range(2)
-    ]
+
+    def head(h):
+        return remote(
+            frame_ref.at[2 + h], head_ref.at[h], head_send.at[h], head_recv.at[h], near[1]
+        )
 
     def fill(dst, tile, half, pick_ref):
         for v in range(VARS):
@@ -572,34 +615,32 @@
         part = me % 2 if order == 0 else 1 - me % 2
         outside_far(part, far_ref, ghost_bf, outside_ref)
 
-        def edge_step(n, carry, part=part):
-            edge_block(
-                n // 2, 2 * part + n % 2, tile_ref, speed_ref, rate_ref, outside_ref, state_ref,
-                up_ref,
+        for step in range(2):
+            half = jnp.where(part == 1, 1 - step, step)
+            group = 2 * part + half
+
+            def edge_step(v, carry, group=group):
+                edge_block(
+                    v, group, tile_ref, speed_ref, rate_ref, outside_ref, state_ref, up_ref
+                )
+                return carry
+
+            lax.fori_loop(0, VARS, edge_step, 0)
+            within = (
+                pl.ds(pl.multiple_of(LANES * group, LANES), LANES)
+                if step == 0
+                else pl.ds(pl.multiple_of(2 * LANES * part, 2 * LANES), 2 * LANES)
             )
-            return carry
-
-        lax.fori_loop(0, 2 * VARS, edge_step, 0)
-        within = pl.ds(pl.multiple_of(2 * LANES * part, 2 * LANES), 2 * LANES)
-        pick_a[...] = jnp.dot(
-            up_ref[:, within], hot_ref[1 - part, within, :], preferred_element_type=F32
-        )
-        for half in range(2):
-            fill(
-                jnp.where(part == 1, TILES, 2) + half, 2 * (1 - part) + half, half, pick_a
+            cols = pl.ds(pl.multiple_of(LANES * half, LANES), LANES)
+            pick_a[:, 0:LANES] = jnp.dot(
+                up_ref[:, within], hot_ref[1 - part, within, cols], preferred_element_type=F32
             )
-            pl.when((part == 1) & jnp.logical_not(last))(tails[half].start)
-            pl.when((part == 0) & jnp.logical_not(first))(heads[half].start)
-
-    total, behind = gathered(z_copies, row_sum, z_buf, z_at, behind)
-    plane_sum[...] = total
-    y_copies = [
-        remote(
-            plane_sum, y_buf.at[k - 1], y_send.at[k - 1], y_recv.at[k - 1],
-            (me + k * ROW_OF * SIDE) % devices,
-        )
-        for k in range(1, SIDE)
-    ]
+            fill(jnp.where(part == 1, TILES, 2) + half, 2 * (1 - part) + half, 0, pick_a)
+            pl.when((part == 1) & jnp.logical_not(last))(tail(half).start)
+            pl.when((part == 0) & jnp.logical_not(first))(head(half).start)
+
+    pl.when(jnp.logical_not(early))(own_tables)
+    gathered(z_copies, row_sum, z_buf, z_at, plane_sum)
     for k in range(1, SIDE):
         pl.when(y_at + k < SIDE)(y_copies[k - 1].start)
 
@@ -616,6 +657,7 @@
         for half in range(2 if pair < 6 else 1):
             fill(2 * pair + half, 2 * pair + half, half, now)
 
+    behind = behind_ref[...]
     for k in range(1, SIDE):
         pl.when(y_at + k < SIDE)(y_copies[k - 1].wait_send)
         pl.when(y_at >= k)(y_copies[k - 1].wait_recv)
@@ -626,13 +668,13 @@
 
         @pl.when(jnp.logical_not(last))
         def _(half=half):
-            tails[half].wait_send()
-            heads[half].wait_recv()
+            tail(half).wait_send()
+            head(half).wait_recv()
 
         @pl.when(jnp.logical_not(first))
         def _(half=half):
-            heads[half].wait_send()
-            tails[half].wait_recv()
+            head(half).wait_send()
+            tail(half).wait_recv()
 
 
 CHUNK = 64
@@ -656,21 +698,16 @@
     def row_tile(rows):
         parts = [pltpu.roll(frame_ref[tile + c, rows, :], back, 1) for c in range(9)]
         out = [jnp.where(kept, parts[c], parts[c + 1]) for c in range(8)]
-        ends = []
-        for c in range(4):
-            at = head_tile + 5 + c
-            part = pltpu.roll(head_ref[jnp.clip(at, 0, 1), rows, :], head_back, 1)
-            ends.append(jnp.where((at >= 0) & (at < 2), part, 0.0))
+        heads = [pltpu.roll(head_ref[c, rows, :], head_back, 1) for c in range(2)]
+        ends = [
+            jnp.where(head_tile + 5 + c == 0, heads[0], jnp.where(head_tile + 5 + c == 1, heads[1], 0.0))
+            for c in range(4)
+        ]
         for c in range(3):
             out[5 + c] = out[5 + c] + jnp.where(head_kept, ends[c], ends[c + 1])
         return out
 
-    out = row_tile(pl.ds(ROWS, 8))
-    for c in range(8):
-        width = min(LANES, E_NEW - c * LANES)
-        jac_ref[0:1, c * LANES : c * LANES + width] = out[c][0:1, :width]
-    copies = [pltpu.make_async_copy(jac_ref, jac_hbm, sems.at[ROWS // CHUNK])]
-    copies[0].start()
+    copies = []
     for chunk in range(ROWS // CHUNK):
         for n in range(CHUNK // 8):
             row = chunk * CHUNK + 8 * n
@@ -682,6 +719,12 @@
         copy = pltpu.make_async_copy(out_ref.at[rows], out_hbm.at[rows], sems.at[chunk])
         copy.start()
         copies.append(copy)
+    out = row_tile(pl.ds(ROWS, 8))
+    for c in range(8):
+        width = min(LANES, E_NEW - c * LANES)
+        jac_ref[0:1, c * LANES : c * LANES + width] = out[c][0:1, :width]
+    copies.append(pltpu.make_async_copy(jac_ref, jac_hbm, sems.at[ROWS // CHUNK]))
+    copies[-1].start()
     for copy in copies:
         copy.wait()
 
@@ -734,10 +777,11 @@
             pltpu.VMEM((1, LANES), jnp.int32),
             pltpu.VMEM((1, LANES), jnp.int32),
             pltpu.VMEM((1, LANES), jnp.int32),
+            pltpu.VMEM((1, LANES), jnp.int32),
             dma((6,)), dma((GROUPS,)), dma((4,)), dma((4,)), dma((ROW_OF - 1,)),
             dma((ROW_OF - 1,)), dma((SIDE - 1,)), dma((SIDE - 1,)), dma((SIDE - 1,)),
             dma((SIDE - 1,)),
-            dma((2,)), dma((2,)), dma((2,)), dma((2,)),
+            dma((2,)), dma((2,)), dma((2,)), dma((2,)), pltpu.SemaphoreType.REGULAR,
         ],
         compiler_params=pltpu.CompilerParams(
             collective_id=0, has_side_effects=True, vmem_limit_bytes=28 << 20

time: 23.6 us -> 22.8 us (0.966)
  Pallas kernels: 22.9 us -> 22.1 us
    pallas_call x1, Pallas kernels: 21.3 us -> 20.5 us  [shards(): pl.pallas_call(kernel, out_shape=(jax.ShapeDtypeStruct((TILES + 2, FRAME,...]
where the time goes in v5:
time: 22.8 us; the launch traced here: 22.7 us
  Pallas kernels  22.1 us (97%)
  between operations  0.64 us (3%)
    pallas_call x1, Pallas kernels, shards(): pl.pallas_call(kernel, out_shape=(jax.ShapeDtypeStruct((TILES + 2, FRAME,...  20.5 us
    pallas_call x1, Pallas kernels, shards(): pl.pallas_call(place_kernel, out_shape=(jax.ShapeDtypeStruct((ROWS, E_NEW...  1.56 us

profile of v5, /device:TPU:24, one launch (start us, length us, event | category | flops | bytes accessed | tf_op | source)
XLA Modules:
  0.0 22.7 jit_solution(2115344520039245134)
XLA Ops:
  0.6 20.5 %step.1 = (f32[15,328,128]{2,1,0:T(8,128)S(1)}, f32[2,328,128]{2,1,0:T(8,128)S(1)}, s32[2,128]{1,0:T(2,128)S(1)}) custom-call(f32[320,512]{1,0:T(8,128)} %bitcast.5, f32[1,512]{1,0:T(1,128)} %bitcast.6, f32[3,5]{1,0:T(4,128)} %speed_hbm.1, s32[1,512]{1,0:T(1,128)} %bitcast.7, s32[384]{0:T(512)} %send_hbm.1, s32[6,512]{1,0:T(8,128)} %source_hbm.1, ...), custom_call_target="tpu_custom_call" | custom-call | tf_op jit(solution)/shard_map/step/pallas_call | solution.py:741
  21.1 1.6 %place.1 = (f32[320,960]{1,0:T(8,128)}, f32[1,960]{1,0:T(1,128)}) custom-call(f32[15,328,128]{2,1,0:T(8,128)S(1)} %get-tuple-element.7.frame_ref, f32[2,328,128]{2,1,0:T(8,128)S(1)} %get-tuple-element.8.head_ref, s32[2,128]{1,0:T(2,128)S(1)} %get-tuple-element.9.info_ref), custom_call_target="tpu_custom_call" | custom-call | tf_op jit(solution)/shard_map/place/pallas_call | solution.py:794

commit v6 on v5

--- a/solution.py
+++ b/solution.py
@@ -426,6 +426,34 @@
 
 TILES = 13
 FRAME = ROWS + 8
+PACKED = ROWS // 4 * 3 + 8
+
+
+def pack(frame_ref, tile, pack_ref, part):
+    lane = lax.broadcasted_iota(jnp.int32, (8, LANES), 1)
+    unused = jnp.where(part == 1, lane, LANES - 1 - lane) < 32
+    for n in range(ROWS // 32):
+        fourth = frame_ref[tile, 32 * n + 24 : 32 * n + 32, :]
+        for j in range(3):
+            rows = frame_ref[tile, 32 * n + 8 * j : 32 * n + 8 * j + 8, :]
+            pack_ref[part, 24 * n + 8 * j : 24 * n + 8 * j + 8, :] = jnp.where(
+                unused, pltpu.roll(fourth, 96 - 32 * j, 1), rows
+            )
+    pack_ref[part, PACKED - 8 : PACKED, :] = frame_ref[tile, ROWS:FRAME, :]
+
+
+def unpack(land_ref, part, dst_ref, tile):
+    lane = lax.broadcasted_iota(jnp.int32, (8, LANES), 1)
+    for n in range(ROWS // 32):
+        rows = [land_ref[part, 24 * n + 8 * j : 24 * n + 8 * j + 8, :] for j in range(3)]
+        turned = [pltpu.roll(rows[j], 32 + 32 * j, 1) for j in range(3)]
+        for j in range(3):
+            dst_ref[tile, 32 * n + 8 * j : 32 * n + 8 * j + 8, :] = rows[j]
+        dst_ref[tile, 32 * n + 24 : 32 * n + 32, :] = jnp.where(
+            lane < 32 + 32 * part, turned[0],
+            jnp.where(lane < 64 + 32 * part, turned[1], turned[2]),
+        )
+    dst_ref[tile, ROWS:FRAME, :] = land_ref[part, PACKED - 8 : PACKED, :]
 
 
 def kernel(
@@ -433,7 +461,7 @@
     frame_ref, head_ref, info_ref,
     jac_ref, speed_ref, flag_ref, send_ref, source_ref, modes_ref,
     tile_ref, trace_ref, out_buf, ghost_ref, ghost_bf, outside_ref, rate_ref, state_ref, up_ref,
-    start_ref, aux_ref, coef_ref, hot_ref, pick_a, pick_b, line_ref, far_ref,
+    start_ref, aux_ref, coef_ref, hot_ref, pick_a, pick_b, line_ref, far_ref, pack_ref, land_ref,
     row_buf, z_buf, y_buf, mine, row_sum, plane_sum, behind_ref,
     small_sems, fetch_sems, send_sems, recv_sems, row_send, row_recv, z_send, z_recv,
     y_send, y_recv,
@@ -593,15 +621,18 @@
     split_ghost(ghost_ref, ghost_bf)
     first, last = me == 0, me == devices - 1
 
-    def tail(h):
-        return remote(
-            frame_ref.at[TILES + h], frame_ref.at[h], tail_send.at[h], tail_recv.at[h], near[2]
-        )
-
-    def head(h):
-        return remote(
-            frame_ref.at[2 + h], head_ref.at[h], head_send.at[h], head_recv.at[h], near[1]
-        )
+    outer_tail = remote(
+        frame_ref.at[TILES + 1], frame_ref.at[1], tail_send.at[1], tail_recv.at[1], near[2]
+    )
+    outer_head = remote(
+        frame_ref.at[2], head_ref.at[0], head_send.at[0], head_recv.at[0], near[1]
+    )
+    inner_tail = remote(
+        pack_ref.at[1], land_ref.at[1], tail_send.at[0], tail_recv.at[0], near[2]
+    )
+    inner_head = remote(
+        pack_ref.at[0], land_ref.at[0], head_send.at[1], head_recv.at[1], near[1]
+    )
 
     def fill(dst, tile, half, pick_ref):
         for v in range(VARS):
@@ -636,8 +667,13 @@
                 up_ref[:, within], hot_ref[1 - part, within, cols], preferred_element_type=F32
             )
             fill(jnp.where(part == 1, TILES, 2) + half, 2 * (1 - part) + half, 0, pick_a)
-            pl.when((part == 1) & jnp.logical_not(last))(tail(half).start)
-            pl.when((part == 0) & jnp.logical_not(first))(head(half).start)
+            if step == 0:
+                pl.when((part == 1) & jnp.logical_not(last))(outer_tail.start)
+                pl.when((part == 0) & jnp.logical_not(first))(outer_head.start)
+            else:
+                pack(frame_ref, jnp.where(part == 1, TILES, 3), pack_ref, part)
+                pl.when((part == 1) & jnp.logical_not(last))(inner_tail.start)
+                pl.when((part == 0) & jnp.logical_not(first))(inner_head.start)
 
     pl.when(jnp.logical_not(early))(own_tables)
     gathered(z_copies, row_sum, z_buf, z_at, plane_sum)
@@ -664,25 +700,30 @@
         behind = behind + jnp.where(y_at >= k, y_buf[k - 1], 0)
     info_ref[0:1, :] = behind
     info_ref[1:2, :] = total_new.astype(jnp.int32)
-    for half in range(2):
-
-        @pl.when(jnp.logical_not(last))
-        def _(half=half):
-            tail(half).wait_send()
-            head(half).wait_recv()
-
-        @pl.when(jnp.logical_not(first))
-        def _(half=half):
-            head(half).wait_send()
-            tail(half).wait_recv()
+
+    @pl.when(jnp.logical_not(last))
+    def _():
+        outer_tail.wait_send()
+        inner_tail.wait_send()
+        outer_head.wait_recv()
+        inner_head.wait_recv()
+        unpack(land_ref, 0, head_ref, 1)
+
+    @pl.when(jnp.logical_not(first))
+    def _():
+        outer_head.wait_send()
+        inner_head.wait_send()
+        outer_tail.wait_recv()
+        inner_tail.wait_recv()
+        unpack(land_ref, 1, frame_ref, 0)
 
 
 CHUNK = 64
 
 
 def place_kernel(frame_ref, head_ref, info_ref, out_hbm, jac_hbm, out_ref, jac_ref, sems):
-    shift = 7 * jnp.max(info_ref[0:1, :])
-    size = jnp.max(info_ref[1:2, :])
+    shift = 7 * info_ref[0, 0]
+    size = info_ref[1, 0]
     begin = 2 * LANES - shift
     tile = begin // LANES
     turn_by = begin - tile * LANES
@@ -771,6 +812,8 @@
             pltpu.VMEM((2 * ROWS, 2 * LANES), F32),
             pltpu.VMEM((VARS, 64, LANES), F32),
             pltpu.VMEM((6, E_DEV, E_DEV), BF16),
+            pltpu.VMEM((2, PACKED, LANES), F32),
+            pltpu.VMEM((2, PACKED, LANES), F32),
             pltpu.VMEM((ROW_OF - 1, 1, LANES), jnp.int32),
             pltpu.VMEM((SIDE - 1, 1, LANES), jnp.int32),
             pltpu.VMEM((SIDE - 1, 1, LANES), jnp.int32),

time: 22.8 us -> 22.3 us (0.978)
  Pallas kernels: 22.1 us -> 21.5 us
    pallas_call x1, Pallas kernels: 20.5 us -> 20.2 us  [shards(): pl.pallas_call(kernel, out_shape=(jax.ShapeDtypeStruct((TILES + 2, FRAME,...]
where the time goes in v6:
time: 22.3 us; the launch traced here: 22.1 us
  Pallas kernels  21.5 us (96%)
  between operations  0.64 us (3%)
    pallas_call x1, Pallas kernels, shards(): pl.pallas_call(kernel, out_shape=(jax.ShapeDtypeStruct((TILES + 2, FRAME,...  20.2 us
    pallas_call x1, Pallas kernels, shards(): pl.pallas_call(place_kernel, out_shape=(jax.ShapeDtypeStruct((ROWS, E_NEW...  1.34 us

profile of v6, /device:TPU:24, one launch (start us, length us, event | category | flops | bytes accessed | tf_op | source)
XLA Modules:
  0.0 22.1 jit_solution(1418176312062582567)
XLA Ops:
  0.6 20.2 %step.1 = (f32[15,328,128]{2,1,0:T(8,128)S(1)}, f32[2,328,128]{2,1,0:T(8,128)S(1)}, s32[2,128]{1,0:T(2,128)S(1)}) custom-call(f32[320,512]{1,0:T(8,128)} %bitcast.5, f32[1,512]{1,0:T(1,128)} %bitcast.6, f32[3,5]{1,0:T(4,128)} %speed_hbm.1, s32[1,512]{1,0:T(1,128)} %bitcast.7, s32[384]{0:T(512)} %send_hbm.1, s32[6,512]{1,0:T(8,128)} %source_hbm.1, ...), custom_call_target="tpu_custom_call" | custom-call | tf_op jit(solution)/shard_map/step/pallas_call | solution.py:782
  20.8 1.3 %place.1 = (f32[320,960]{1,0:T(8,128)}, f32[1,960]{1,0:T(1,128)}) custom-call(f32[15,328,128]{2,1,0:T(8,128)S(1)} %get-tuple-element.7.frame_ref, f32[2,328,128]{2,1,0:T(8,128)S(1)} %get-tuple-element.8.head_ref, s32[2,128]{1,0:T(2,128)S(1)} %get-tuple-element.9.info_ref), custom_call_target="tpu_custom_call" | custom-call | tf_op jit(solution)/shard_map/place/pallas_call | solution.py:837

commit v7 on v6

--- a/solution.py
+++ b/solution.py
@@ -204,9 +204,9 @@
             + (far >= 2 * SLOTS).astype(jnp.int32)
             + (far >= 3 * SLOTS).astype(jnp.int32)
         )
-        far_ref[f] = one_hot(
-            jnp.where(far >= 0, far + (LANES - SLOTS) * slot, -1), E_DEV, E_DEV
-        )
+        hot = one_hot(jnp.where(far >= 0, far + (LANES - SLOTS) * slot, -1), E_DEV, E_DEV)
+        for g in range(GROUPS):
+            far_ref[g, :, f * LANES : (f + 1) * LANES] = hot[:, g * LANES : (g + 1) * LANES]
 
 
 def split_ghost(ghost_ref, ghost_bf):
@@ -216,11 +216,12 @@
         ghost_bf[80:160, slot * LANES : (slot + 1) * LANES] = rest
 
 
-def outside_far(half, far_ref, ghost_bf, outside_ref):
-    cols = pl.ds(pl.multiple_of(2 * LANES * half, 2 * LANES), 2 * LANES)
+def outside_far(group, far_ref, ghost_bf, outside_ref):
+    cols = pl.ds(pl.multiple_of(LANES * group, LANES), LANES)
+    total = jnp.dot(ghost_bf[...], far_ref[group], preferred_element_type=F32)
     for f in range(6):
-        total = jnp.dot(ghost_bf[...], far_ref[f, :, cols], preferred_element_type=F32)
-        outside_ref[f, :, cols] += total[0:80] + total[80:160]
+        part = slice(f * LANES, (f + 1) * LANES)
+        outside_ref[f, :, cols] += total[0:80, part] + total[80:160, part]
 
 
 def coefs_of(d, v, speed_ref, hi, lo):
@@ -277,8 +278,8 @@
 
 
 def edge_block(v, g, tile_ref, speed_ref, rate_ref, outside_ref, state_ref, up_ref):
-    base = pl.multiple_of(64 * v, 64)
-    face = pl.multiple_of(16 * v, 16)
+    base = 64 * v
+    face = 16 * v
     cols = pl.ds(pl.multiple_of(g * LANES, LANES), LANES)
     step = rate_ref[2:3, cols]
     low = low_half((8, LANES))
@@ -313,8 +314,8 @@
         total[2 * k + 1] += jnp.where(low, 0.0, bound)
     for t in range(4):
         high, rest = split2(jnp.concatenate(total[2 * t : 2 * t + 2], axis=0))
-        up_ref[pl.ds(pl.multiple_of(base + 16 * t, 16), 16), cols] = high
-        up_ref[pl.ds(pl.multiple_of(ROWS + base + 16 * t, 16), 16), cols] = rest
+        up_ref[base + 16 * t : base + 16 * t + 16, cols] = high
+        up_ref[ROWS + base + 16 * t : ROWS + base + 16 * t + 16, cols] = rest
 
 
 def refine_tables(flag_ref, jac_ref, start_ref, aux_ref):
@@ -476,6 +477,7 @@
     row_mates = [me - row_at + (row_at + k) % ROW_OF for k in range(1, ROW_OF)]
     z_mates = [me + ROW_OF * ((z_at + k) % SIDE - z_at) for k in range(1, SIDE)]
     early = me % (ROW_OF * SIDE) < 2
+    idle = early | (me % (ROW_OF * SIDE) >= ROW_OF * SIDE - 2)
     awaited = me >= devices - 4
     barrier = pltpu.get_barrier_semaphore()
     for b, partner in enumerate(near):
@@ -576,7 +578,7 @@
     ]
     pl.when(awaited)(near_work)
     pl.when(jnp.logical_not(early))(inner_work)
-    pl.when(early)(own_tables)
+    pl.when(idle)(own_tables)
 
     @pl.when(me < 2)
     def _():
@@ -644,19 +646,16 @@
 
     for order in range(2):
         part = me % 2 if order == 0 else 1 - me % 2
-        outside_far(part, far_ref, ghost_bf, outside_ref)
 
         for step in range(2):
             half = jnp.where(part == 1, 1 - step, step)
             group = 2 * part + half
-
-            def edge_step(v, carry, group=group):
+            outside_far(group, far_ref, ghost_bf, outside_ref)
+
+            for v in range(VARS):
                 edge_block(
                     v, group, tile_ref, speed_ref, rate_ref, outside_ref, state_ref, up_ref
                 )
-                return carry
-
-            lax.fori_loop(0, VARS, edge_step, 0)
             within = (
                 pl.ds(pl.multiple_of(LANES * group, LANES), LANES)
                 if step == 0
@@ -675,7 +674,7 @@
                 pl.when((part == 1) & jnp.logical_not(last))(inner_tail.start)
                 pl.when((part == 0) & jnp.logical_not(first))(inner_head.start)
 
-    pl.when(jnp.logical_not(early))(own_tables)
+    pl.when(jnp.logical_not(idle))(own_tables)
     gathered(z_copies, row_sum, z_buf, z_at, plane_sum)
     for k in range(1, SIDE):
         pl.when(y_at + k < SIDE)(y_copies[k - 1].start)
@@ -811,7 +810,7 @@
             pltpu.VMEM((2 * ROWS, 2 * LANES), F32),
             pltpu.VMEM((2 * ROWS, 2 * LANES), F32),
             pltpu.VMEM((VARS, 64, LANES), F32),
-            pltpu.VMEM((6, E_DEV, E_DEV), BF16),
+            pltpu.VMEM((GROUPS, E_DEV, 6 * LANES), BF16),
             pltpu.VMEM((2, PACKED, LANES), F32),
             pltpu.VMEM((2, PACKED, LANES), F32),
             pltpu.VMEM((ROW_OF - 1, 1, LANES), jnp.int32),

time: 22.3 us -> 22.1 us (level)
  no operation moved by 1% of the time
where the time goes in v7:
time: 22.1 us; the launch traced here: 22 us
  Pallas kernels  21.3 us (96%)
  between operations  0.64 us (3%)
    pallas_call x1, Pallas kernels, shards(): pl.pallas_call(kernel, out_shape=(jax.ShapeDtypeStruct((TILES + 2, FRAME,...  20 us
    pallas_call x1, Pallas kernels, shards(): pl.pallas_call(place_kernel, out_shape=(jax.ShapeDtypeStruct((ROWS, E_NEW...  1.34 us

profile of v7, /device:TPU:24, one launch (start us, length us, event | category | flops | bytes accessed | tf_op | source)
XLA Modules:
  0.0 22.0 jit_solution(3015728064614022477)
XLA Ops:
  0.6 20.0 %step.1 = (f32[15,328,128]{2,1,0:T(8,128)S(1)}, f32[2,328,128]{2,1,0:T(8,128)S(1)}, s32[2,128]{1,0:T(2,128)S(1)}) custom-call(f32[320,512]{1,0:T(8,128)} %bitcast.5, f32[1,512]{1,0:T(1,128)} %bitcast.6, f32[3,5]{1,0:T(4,128)} %speed_hbm.1, s32[1,512]{1,0:T(1,128)} %bitcast.7, s32[384]{0:T(512)} %send_hbm.1, s32[6,512]{1,0:T(8,128)} %source_hbm.1, ...), custom_call_target="tpu_custom_call" | custom-call | tf_op jit(solution)/shard_map/step/pallas_call | solution.py:781
  20.6 1.3 %place.1 = (f32[320,960]{1,0:T(8,128)}, f32[1,960]{1,0:T(1,128)}) custom-call(f32[15,328,128]{2,1,0:T(8,128)S(1)} %get-tuple-element.7.frame_ref, f32[2,328,128]{2,1,0:T(8,128)S(1)} %get-tuple-element.8.head_ref, s32[2,128]{1,0:T(2,128)S(1)} %get-tuple-element.9.info_ref), custom_call_target="tpu_custom_call" | custom-call | tf_op jit(solution)/shard_map/place/pallas_call | solution.py:836

commit v8 on v7

--- a/solution.py
+++ b/solution.py
@@ -734,17 +734,16 @@
     head_kept = lane < LANES - head_turn
     back = (LANES - turn_by) % LANES
     head_back = (LANES - head_turn) % LANES
+    picked = [jnp.where(head_kept, head_tile + 5 + c, head_tile + 6 + c) for c in range(3)]
+    zeroth = [p == 0 for p in picked]
+    oneth = [p == 1 for p in picked]
 
     def row_tile(rows):
         parts = [pltpu.roll(frame_ref[tile + c, rows, :], back, 1) for c in range(9)]
         out = [jnp.where(kept, parts[c], parts[c + 1]) for c in range(8)]
         heads = [pltpu.roll(head_ref[c, rows, :], head_back, 1) for c in range(2)]
-        ends = [
-            jnp.where(head_tile + 5 + c == 0, heads[0], jnp.where(head_tile + 5 + c == 1, heads[1], 0.0))
-            for c in range(4)
-        ]
         for c in range(3):
-            out[5 + c] = out[5 + c] + jnp.where(head_kept, ends[c], ends[c + 1])
+            out[5 + c] += jnp.where(zeroth[c], heads[0], jnp.where(oneth[c], heads[1], 0.0))
         return out
 
     copies = []

time: 22.1 us -> 22.1 us (level)
  no operation moved by 1% of the time
where the time goes in v8:
time: 22.1 us; the launch traced here: 22 us
  Pallas kernels  21.3 us (96%)
  between operations  0.64 us (3%)
    pallas_call x1, Pallas kernels, shards(): pl.pallas_call(kernel, out_shape=(jax.ShapeDtypeStruct((TILES + 2, FRAME,...  20 us
    pallas_call x1, Pallas kernels, shards(): pl.pallas_call(place_kernel, out_shape=(jax.ShapeDtypeStruct((ROWS, E_NEW...  1.34 us

profile of v8, /device:TPU:24, one launch (start us, length us, event | category | flops | bytes accessed | tf_op | source)
XLA Modules:
  0.0 22.0 jit_solution(9769914110083187106)
XLA Ops:
  0.6 20.0 %step.1 = (f32[15,328,128]{2,1,0:T(8,128)S(1)}, f32[2,328,128]{2,1,0:T(8,128)S(1)}, s32[2,128]{1,0:T(2,128)S(1)}) custom-call(f32[320,512]{1,0:T(8,128)} %bitcast.5, f32[1,512]{1,0:T(1,128)} %bitcast.6, f32[3,5]{1,0:T(4,128)} %speed_hbm.1, s32[1,512]{1,0:T(1,128)} %bitcast.7, s32[384]{0:T(512)} %send_hbm.1, s32[6,512]{1,0:T(8,128)} %source_hbm.1, ...), custom_call_target="tpu_custom_call" | custom-call | tf_op jit(solution)/shard_map/step/pallas_call | solution.py:780
  20.6 1.3 %place.1 = (f32[320,960]{1,0:T(8,128)}, f32[1,960]{1,0:T(1,128)}) custom-call(f32[15,328,128]{2,1,0:T(8,128)S(1)} %get-tuple-element.7.frame_ref, f32[2,328,128]{2,1,0:T(8,128)S(1)} %get-tuple-element.8.head_ref, s32[2,128]{1,0:T(2,128)S(1)} %get-tuple-element.9.info_ref), custom_call_target="tpu_custom_call" | custom-call | tf_op jit(solution)/shard_map/place/pallas_call | solution.py:835
